TPU v7x, 128 devices: a whole 4x4x4 slice. The times are simulated.
128 devices in a mesh: bl: 32 (over z_hi, y, x), bp: 4 (over z_lo, core).
Axes of the slice: x: 4, y: 4, z: 4 (z_hi: 2, z_lo: 2; z = z_hi * 2 + z_lo), core: 2. Of those that a mesh axis runs over, the one named last changes fastest.
Arguments:
- inverse_cov: float32 [32, 1024, 1024], P('bl', 'bp'), may hold values from -1 to 12, as said below
- channel_keep_mask: int32 [32, 1024], P('bl'), may hold values 0 or 1
- partner_ids: int32 [32, 2], P('bl'), may hold values from -1 to 31, as said below
- band_starts: int32 [2, 64], replicated, may hold values from 0 to 384
Outputs:
- fisher: float32 [2, 64, 64], P(None, 'bp', 'bl')
Inputs may be any that keep to these rules, and one draw needn't show every extreme that they name: partner_ids[i, k] is -1 for an empty slot, else the index of a baseline whose group, its index // 1, lies 1 to 4 groups after the group of baseline i, counted cyclically over the 32 groups; in every draw some baseline has all 2 slots filled. Each inverse_cov[i] is symmetric.
All inputs are finite; a program needn't handle non-finite values. No bound on the sum of `channel_keep_mask` on one device may be relied on, other than what follows from the above.
Results may differ from a plain program's by a relative error of at most 0.0003.
Values sent between devices are 32-bit elements; how exact they have to be, the bound alone decides.
A program may use at most 128 MiB of HBM per device.

v0:
```python
from functools import partial

import jax
import jax.numpy as jnp
from jax import lax
from jax.sharding import PartitionSpec as P

WINDOW_LENGTH = 128
GROUP_REACH = 4


highest = lax.Precision.HIGHEST


def laid_out(tiles, dim):
    dims = list(tiles.shape[1:])
    dims[dim] *= tiles.shape[0]
    return jnp.moveaxis(tiles, 0, dim).reshape(dims)


def copy_for_each(x, axis):
    copies = jnp.broadcast_to(x, (lax.axis_size(axis), *x.shape))
    return lax.all_to_all(copies, axis, split_axis=0, concat_axis=0, tiled=True)


def collect(x, axis, dim):
    return laid_out(copy_for_each(x, axis), dim)


def passed_along(value, axis, steps):
    count = lax.axis_size(axis)
    pairs = [(source, (source + steps) % count) for source in range(count)]
    return lax.ppermute(value, axis, pairs)


def split_up(x, dim, length):
    dims = x.shape
    tiles = x.reshape(*dims[:dim], length, dims[dim] // length, *dims[dim + 1 :])
    return jnp.moveaxis(tiles, dim, 0)


def sent_and_summed(x, axis, dim):
    length = lax.axis_size(axis)
    tiles = lax.all_to_all(split_up(x, dim, length), axis, 0, 0, tiled=True)
    return jnp.sum(tiles, axis=0)


def kernel_stack(first_band, band_count, window):
    channel_pos = jnp.arange(window, dtype=jnp.float32)
    spread = jnp.abs(channel_pos[:, None] - channel_pos[None, :])
    band_ids = first_band + jnp.arange(band_count, dtype=jnp.int32)
    length = 1.0 + (band_ids % 4).astype(jnp.float32)
    return jnp.exp(-spread[None, :, :] / length[:, None, None])


def project_turned(panel_block, starts, kernels):
    window = kernels.shape[1]
    window_rows = jax.vmap(
        lambda row_start: lax.dynamic_slice_in_dim(panel_block, row_start, window, 0)
    )(starts)
    return jnp.einsum(
        "apq,aqc->acp", kernels, window_rows, precision=highest, preferred_element_type=jnp.float32
    )


def row_windows(turned, starts, window):

    def one_matrix(matrix):
        return jax.vmap(lambda row_start: lax.dynamic_slice_in_dim(matrix, row_start, window, 0))(
            starts
        )

    return jax.vmap(one_matrix)(turned)


def take_member(received, team_element):
    return lax.dynamic_index_in_dim(received, team_element, 0, keepdims=False)


def contract(turned, block_starts, own_windows):
    partner_windows = row_windows(turned, block_starts, own_windows.shape[2])
    return jnp.einsum(
        "abqp,bapq->ab",
        partner_windows,
        own_windows,
        precision=highest,
        preferred_element_type=jnp.float32,
    )


def block_step(
    block_idx, own_panel, all_start, all_kernels, my_start, projections, presence, block_width
):
    block_begin = block_idx * block_width
    block_starts = lax.dynamic_slice_in_dim(all_start, block_begin, block_width)
    block_kernels = lax.dynamic_slice_in_dim(all_kernels, block_begin, block_width)
    own_turned = project_turned(own_panel, block_starts, block_kernels)
    own_windows = row_windows(own_turned, my_start, all_kernels.shape[1])
    column_sum = jnp.zeros((my_start.shape[0], block_width), jnp.float32)
    for projected, present in zip(projections, presence):
        column_sum = column_sum + lax.cond(
            present,
            partial(contract, projected, block_starts, own_windows),
            partial(jnp.zeros, (my_start.shape[0], block_width), jnp.float32),
        )
    return column_sum


def body(inverse_cov, channel_keep_mask, partner_ids, band_starts):
    local_count, shard_rows, channels = inverse_cov.shape
    panel_width = channels // 2
    window = WINDOW_LENGTH
    band_total = band_starts.shape[1]
    antenna_pair_sets = lax.axis_size("bl")
    owners = lax.axis_size("bp")
    cycle_index = lax.axis_index("bl")
    band_share = band_total // owners
    first_band = lax.axis_index("bp") * band_share
    row_first = lax.axis_index("bp") * shard_rows
    half_start = row_first // panel_width * panel_width
    flag_marks = channel_keep_mask.astype(jnp.float32)
    block_part = lax.dynamic_slice_in_dim(inverse_cov, half_start, panel_width, 2)
    row_marks = lax.dynamic_slice_in_dim(flag_marks, row_first, shard_rows, 1)
    column_marks = lax.dynamic_slice_in_dim(flag_marks, half_start, panel_width, 1)
    masked = block_part * row_marks[:, :, None] * column_marks[:, None, :]
    full_shape = (local_count, 2, panel_width, panel_width)
    own_panels = collect(masked, "bp", 1).reshape(full_shape)
    arrived = [
        passed_along(own_panels, "bl", -number_of_hops)
        for number_of_hops in range(1, GROUP_REACH + 1)
    ]
    pickers = [partial(take_member, received) for received in arrived]
    my_kernels = kernel_stack(first_band, band_share, window)
    all_kernels = kernel_stack(0, band_total, window)
    block_width = 4
    block_count = band_total // block_width
    halves = [jnp.zeros((band_share, band_total), jnp.float32) for half_index in range(2)]
    targets = partner_ids[0]
    presence_all = targets >= 0
    hop_index = jnp.clip(
        (targets // local_count - cycle_index) % antenna_pair_sets - 1, 0, GROUP_REACH - 1
    )
    team_element = jnp.clip(targets % local_count, 0, local_count - 1)
    summed_panels = jnp.zeros((2, panel_width, panel_width), jnp.float32)
    for slot_index in range(targets.shape[0]):
        summed_panels = summed_panels + jnp.where(
            presence_all[slot_index],
            lax.switch(hop_index[slot_index], pickers, team_element[slot_index]),
            0.0,
        )
    for half_index in range(2):
        all_start = band_starts[half_index]
        my_start = lax.dynamic_slice_in_dim(all_start, first_band, band_share)
        projections = [project_turned(summed_panels[half_index], my_start, my_kernels)]
        presence = [jnp.any(presence_all)]
        stepper = partial(
            block_step,
            own_panel=own_panels[0, half_index],
            all_start=all_start,
            all_kernels=all_kernels,
            my_start=my_start,
            projections=projections,
            presence=presence,
            block_width=block_width,
        )
        block_sums = lax.map(stepper, jnp.arange(block_count, dtype=jnp.int32))
        running_totals = jnp.transpose(block_sums, (1, 0, 2)).reshape(band_share, band_total)
        halves[half_index] = halves[half_index] + running_totals
    normalizer = 1.0 / (4 * local_count * antenna_pair_sets * window)
    partial_fisher = jnp.stack(halves) * normalizer
    return sent_and_summed(partial_fisher, "bl", 2)


def solution(mesh):
    placed = (P("bl", "bp", None), P("bl", None), P("bl", None), P())
    return jax.shard_map(
        body, mesh=mesh, in_specs=placed, out_specs=P(None, "bp", "bl"), check_vma=False
    )
```

profile of v0, /device:TPU:1, one launch (start us, length us, event | category | flops | bytes accessed | tf_op | source)
XLA Modules:
  0.0 1333.7 jit_solution(7057089058582549844)
XLA Ops:
  3.5 5.8 all-to-all-start
  9.3 24.8 %all-to-all-done = f32[4,1,256,512]{3,2,1,0:T(8,128)} async-done(((f32[4,1,256,512]{3,2,1,0:T(8,128)}), f32[4,1,256,512]{3,2,1,0:T(8,128)}, u32[]{:S(2)}, u32[]{:S(2)}) %all-to-all-start) | async-done | bytes 2097184 | tf_op jit(solution)/shard_map/all_to_all | solution.py:23
  34.1 8.4 collective-permute-start
  52.7 104.4 %collective-permute-done = f32[1,2,512,512]{3,2,1,0:T(8,128)} collective-permute-done((f32[1,2,512,512]{3,2,1,0:T(8,128)}, f32[1,2,512,512]{3,2,1,0:T(8,128)}, u32[]{:S(2)}, u32[]{:S(2)}) %collective-permute-start) | collective-permute-done | bytes 2097184 | tf_op jit(solution)/shard_map/ppermute | solution.py:33
  171.1 33.6 %while.30 = (s32[]{:T(128)}, f32[512,512]{1,0:T(8,128)S(1)}, s32[16,2]{0,1:T(2,128)S(1)}, f32[16,128,512]{2,1,0:T(8,128)}, s32[]{:T(128)}) while((s32[]{:T(128)}, f32[512,512]{1,0:T(8,128)S(1)}, s32[16,2]{0,1:T(2,128)S(1)}, f32[16,128,512]{2,1,0:T(8,128)}, s32[]{:T(128)}) %tuple.219), condition=%wide.while_cond.2, body=%wide.while_body.2.sunk | while | flops 2 | bytes 525401 | solution.py:59
  204.7 8.6 fusion.17
  217.7 518.9 %while.27 = (s32[]{:T(128)}, f32[16,16,4]{1,2,0:T(4,128)S(1)}, pred[]{:T(512)}, s32[16]{0:T(128)S(1)}, s32[64]{0:T(128)S(1)}, /*index=5*/f32[512,512]{1,0:T(8,12...) while((s32[]{:T(128)}, f32[16,16,4]{1,2,0:T(4,128)S(1)}, ...), condition=%wide.region_12.13_spmd, body=%wide.region_9.12_spmd.sunk | while | flops 404750400 | bytes 38540844 | solution.py:166
  219.1 8.5 while.32
  231.0 19.3 %conditional.8 = (f32[1,16,4]{1,2,0:T(4,128)S(1)}) conditional(s32[]{:T(128)} %convert_element_type.36, () %tuple.195, (s32[4]{0:T(128)S(1)}, f32[16,512,128]{2,0,1:T(8,128)}, s32[16]{0:T(128)S(1)}, f32[4,512,128]{2,1,0:T(8,128)S(1)}) %tuple.197), branch_computations={%region_10.10_spmd, %region_11.11_spmd} | conditional | flops 2097188 | bytes 35652680 | solution.py:101
  251.5 8.5 while.32
  263.4 19.3 %conditional.8 = (f32[1,16,4]{1,2,0:T(4,128)S(1)}) conditional(s32[]{:T(128)} %convert_element_type.36, () %tuple.195, (s32[4]{0:T(128)S(1)}, f32[16,512,128]{2,0,1:T(8,128)}, s32[16]{0:T(128)S(1)}, f32[4,512,128]{2,1,0:T(8,128)S(1)}) %tuple.197), branch_computations={%region_10.10_spmd, %region_11.11_spmd} | conditional | flops 2097188 | bytes 35652680 | solution.py:101
  283.9 8.5 while.32
  295.9 19.3 %conditional.8 = (f32[1,16,4]{1,2,0:T(4,128)S(1)}) conditional(s32[]{:T(128)} %convert_element_type.36, () %tuple.195, (s32[4]{0:T(128)S(1)}, f32[16,512,128]{2,0,1:T(8,128)}, s32[16]{0:T(128)S(1)}, f32[4,512,128]{2,1,0:T(8,128)S(1)}) %tuple.197), branch_computations={%region_10.10_spmd, %region_11.11_spmd} | conditional | flops 2097188 | bytes 35652680 | solution.py:101
  316.4 8.5 while.32
  328.3 19.3 %conditional.8 = (f32[1,16,4]{1,2,0:T(4,128)S(1)}) conditional(s32[]{:T(128)} %convert_element_type.36, () %tuple.195, (s32[4]{0:T(128)S(1)}, f32[16,512,128]{2,0,1:T(8,128)}, s32[16]{0:T(128)S(1)}, f32[4,512,128]{2,1,0:T(8,128)S(1)}) %tuple.197), branch_computations={%region_10.10_spmd, %region_11.11_spmd} | conditional | flops 2097188 | bytes 35652680 | solution.py:101
  328.3 4.9 gather_fusion
  348.8 8.5 while.32
  360.7 19.3 %conditional.8 = (f32[1,16,4]{1,2,0:T(4,128)S(1)}) conditional(s32[]{:T(128)} %convert_element_type.36, () %tuple.195, (s32[4]{0:T(128)S(1)}, f32[16,512,128]{2,0,1:T(8,128)}, s32[16]{0:T(128)S(1)}, f32[4,512,128]{2,1,0:T(8,128)S(1)}) %tuple.197), branch_computations={%region_10.10_spmd, %region_11.11_spmd} | conditional | flops 2097188 | bytes 35652680 | solution.py:101
  360.7 4.9 gather_fusion
  381.2 8.5 while.32
  393.1 19.3 %conditional.8 = (f32[1,16,4]{1,2,0:T(4,128)S(1)}) conditional(s32[]{:T(128)} %convert_element_type.36, () %tuple.195, (s32[4]{0:T(128)S(1)}, f32[16,512,128]{2,0,1:T(8,128)}, s32[16]{0:T(128)S(1)}, f32[4,512,128]{2,1,0:T(8,128)S(1)}) %tuple.197), branch_computations={%region_10.10_spmd, %region_11.11_spmd} | conditional | flops 2097188 | bytes 35652680 | solution.py:101
  393.1 4.9 gather_fusion
  413.6 8.5 while.32
  425.5 19.3 %conditional.8 = (f32[1,16,4]{1,2,0:T(4,128)S(1)}) conditional(s32[]{:T(128)} %convert_element_type.36, () %tuple.195, (s32[4]{0:T(128)S(1)}, f32[16,512,128]{2,0,1:T(8,128)}, s32[16]{0:T(128)S(1)}, f32[4,512,128]{2,1,0:T(8,128)S(1)}) %tuple.197), branch_computations={%region_10.10_spmd, %region_11.11_spmd} | conditional | flops 2097188 | bytes 35652680 | solution.py:101
  446.0 8.5 while.32
  457.9 19.3 %conditional.8 = (f32[1,16,4]{1,2,0:T(4,128)S(1)}) conditional(s32[]{:T(128)} %convert_element_type.36, () %tuple.195, (s32[4]{0:T(128)S(1)}, f32[16,512,128]{2,0,1:T(8,128)}, s32[16]{0:T(128)S(1)}, f32[4,512,128]{2,1,0:T(8,128)S(1)}) %tuple.197), branch_computations={%region_10.10_spmd, %region_11.11_spmd} | conditional | flops 2097188 | bytes 35652680 | solution.py:101
  478.4 8.5 while.32
  490.4 19.3 %conditional.8 = (f32[1,16,4]{1,2,0:T(4,128)S(1)}) conditional(s32[]{:T(128)} %convert_element_type.36, () %tuple.195, (s32[4]{0:T(128)S(1)}, f32[16,512,128]{2,0,1:T(8,128)}, s32[16]{0:T(128)S(1)}, f32[4,512,128]{2,1,0:T(8,128)S(1)}) %tuple.197), branch_computations={%region_10.10_spmd, %region_11.11_spmd} | conditional | flops 2097188 | bytes 35652680 | solution.py:101
  510.9 8.5 while.32
  522.8 19.3 %conditional.8 = (f32[1,16,4]{1,2,0:T(4,128)S(1)}) conditional(s32[]{:T(128)} %convert_element_type.36, () %tuple.195, (s32[4]{0:T(128)S(1)}, f32[16,512,128]{2,0,1:T(8,128)}, s32[16]{0:T(128)S(1)}, f32[4,512,128]{2,1,0:T(8,128)S(1)}) %tuple.197), branch_computations={%region_10.10_spmd, %region_11.11_spmd} | conditional | flops 2097188 | bytes 35652680 | solution.py:101
  543.3 8.5 while.32
  555.2 19.3 %conditional.8 = (f32[1,16,4]{1,2,0:T(4,128)S(1)}) conditional(s32[]{:T(128)} %convert_element_type.36, () %tuple.195, (s32[4]{0:T(128)S(1)}, f32[16,512,128]{2,0,1:T(8,128)}, s32[16]{0:T(128)S(1)}, f32[4,512,128]{2,1,0:T(8,128)S(1)}) %tuple.197), branch_computations={%region_10.10_spmd, %region_11.11_spmd} | conditional | flops 2097188 | bytes 35652680 | solution.py:101
  575.7 8.4 while.32
  587.6 19.3 %conditional.8 = (f32[1,16,4]{1,2,0:T(4,128)S(1)}) conditional(s32[]{:T(128)} %convert_element_type.36, () %tuple.195, (s32[4]{0:T(128)S(1)}, f32[16,512,128]{2,0,1:T(8,128)}, s32[16]{0:T(128)S(1)}, f32[4,512,128]{2,1,0:T(8,128)S(1)}) %tuple.197), branch_computations={%region_10.10_spmd, %region_11.11_spmd} | conditional | flops 2097188 | bytes 35652680 | solution.py:101
  608.1 8.5 while.32
  620.0 19.3 %conditional.8 = (f32[1,16,4]{1,2,0:T(4,128)S(1)}) conditional(s32[]{:T(128)} %convert_element_type.36, () %tuple.195, (s32[4]{0:T(128)S(1)}, f32[16,512,128]{2,0,1:T(8,128)}, s32[16]{0:T(128)S(1)}, f32[4,512,128]{2,1,0:T(8,128)S(1)}) %tuple.197), branch_computations={%region_10.10_spmd, %region_11.11_spmd} | conditional | flops 2097188 | bytes 35652680 | solution.py:101
  640.5 8.5 while.32
  652.4 19.3 %conditional.8 = (f32[1,16,4]{1,2,0:T(4,128)S(1)}) conditional(s32[]{:T(128)} %convert_element_type.36, () %tuple.195, (s32[4]{0:T(128)S(1)}, f32[16,512,128]{2,0,1:T(8,128)}, s32[16]{0:T(128)S(1)}, f32[4,512,128]{2,1,0:T(8,128)S(1)}) %tuple.197), branch_computations={%region_10.10_spmd, %region_11.11_spmd} | conditional | flops 2097188 | bytes 35652680 | solution.py:101
  672.9 8.5 while.32
  684.9 19.3 %conditional.8 = (f32[1,16,4]{1,2,0:T(4,128)S(1)}) conditional(s32[]{:T(128)} %convert_element_type.36, () %tuple.195, (s32[4]{0:T(128)S(1)}, f32[16,512,128]{2,0,1:T(8,128)}, s32[16]{0:T(128)S(1)}, f32[4,512,128]{2,1,0:T(8,128)S(1)}) %tuple.197), branch_computations={%region_10.10_spmd, %region_11.11_spmd} | conditional | flops 2097188 | bytes 35652680 | solution.py:101
  705.4 8.5 while.32
  717.3 19.3 %conditional.8 = (f32[1,16,4]{1,2,0:T(4,128)S(1)}) conditional(s32[]{:T(128)} %convert_element_type.36, () %tuple.195, (s32[4]{0:T(128)S(1)}, f32[16,512,128]{2,0,1:T(8,128)}, s32[16]{0:T(128)S(1)}, f32[4,512,128]{2,1,0:T(8,128)S(1)}) %tuple.197), branch_computations={%region_10.10_spmd, %region_11.11_spmd} | conditional | flops 2097188 | bytes 35652680 | solution.py:101
  739.1 45.0 %while.31 = (s32[]{:T(128)}, f32[512,512]{1,0:T(8,128)}, s32[16,2]{0,1:T(2,128)S(1)}, f32[16,128,512]{2,1,0:T(8,128)}, s32[]{:T(128)}) while((s32[]{:T(128)}, f32[512,512]{1,0:T(8,128)}, s32[16,2]{0,1:T(2,128)S(1)}, f32[16,128,512]{2,1,0:T(8,128)}, s32[]{:T(128)}) %tuple.213), condition=%wide.while_cond.3, body=%wide.while_body.3.sunk | while | flops 2 | bytes 525401 | solution.py:59
  784.1 8.8 fusion.16
  797.4 457.4 %while.29 = (s32[]{:T(128)}, f32[16,16,4]{1,2,0:T(4,128)S(1)}, pred[]{:T(512)}, s32[16]{0:T(128)S(1)}, s32[64]{0:T(128)S(1)}, /*index=5*/f32[512,512]{1,0:T(8,12...) while((s32[]{:T(128)}, f32[16,16,4]{1,2,0:T(4,128)S(1)}, ...), condition=%wide.region_16.17_spmd, body=%wide.region_13.16_spmd.sunk | while | flops 404750400 | bytes 38540844 | solution.py:166
  806.7 19.3 %conditional.9 = (f32[1,16,4]{1,2,0:T(4,128)S(1)}) conditional(s32[]{:T(128)} %convert_element_type.37, () %tuple.200, (s32[4]{0:T(128)S(1)}, f32[16,512,128]{2,0,1:T(8,128)}, s32[16]{0:T(128)S(1)}, f32[4,512,128]{2,1,0:T(8,128)S(1)}) %tuple.202), branch_computations={%region_14.14_spmd, %region_15.15_spmd} | conditional | flops 2097188 | bytes 35652680 | solution.py:101
  835.2 19.3 %conditional.9 = (f32[1,16,4]{1,2,0:T(4,128)S(1)}) conditional(s32[]{:T(128)} %convert_element_type.37, () %tuple.200, (s32[4]{0:T(128)S(1)}, f32[16,512,128]{2,0,1:T(8,128)}, s32[16]{0:T(128)S(1)}, f32[4,512,128]{2,1,0:T(8,128)S(1)}) %tuple.202), branch_computations={%region_14.14_spmd, %region_15.15_spmd} | conditional | flops 2097188 | bytes 35652680 | solution.py:101
  863.8 19.3 %conditional.9 = (f32[1,16,4]{1,2,0:T(4,128)S(1)}) conditional(s32[]{:T(128)} %convert_element_type.37, () %tuple.200, (s32[4]{0:T(128)S(1)}, f32[16,512,128]{2,0,1:T(8,128)}, s32[16]{0:T(128)S(1)}, f32[4,512,128]{2,1,0:T(8,128)S(1)}) %tuple.202), branch_computations={%region_14.14_spmd, %region_15.15_spmd} | conditional | flops 2097188 | bytes 35652680 | solution.py:101
  892.4 19.3 %conditional.9 = (f32[1,16,4]{1,2,0:T(4,128)S(1)}) conditional(s32[]{:T(128)} %convert_element_type.37, () %tuple.200, (s32[4]{0:T(128)S(1)}, f32[16,512,128]{2,0,1:T(8,128)}, s32[16]{0:T(128)S(1)}, f32[4,512,128]{2,1,0:T(8,128)S(1)}) %tuple.202), branch_computations={%region_14.14_spmd, %region_15.15_spmd} | conditional | flops 2097188 | bytes 35652680 | solution.py:101
  892.4 4.9 gather_fusion.2
  921.0 19.3 %conditional.9 = (f32[1,16,4]{1,2,0:T(4,128)S(1)}) conditional(s32[]{:T(128)} %convert_element_type.37, () %tuple.200, (s32[4]{0:T(128)S(1)}, f32[16,512,128]{2,0,1:T(8,128)}, s32[16]{0:T(128)S(1)}, f32[4,512,128]{2,1,0:T(8,128)S(1)}) %tuple.202), branch_computations={%region_14.14_spmd, %region_15.15_spmd} | conditional | flops 2097188 | bytes 35652680 | solution.py:101
  921.0 4.9 gather_fusion.2
  949.6 19.3 %conditional.9 = (f32[1,16,4]{1,2,0:T(4,128)S(1)}) conditional(s32[]{:T(128)} %convert_element_type.37, () %tuple.200, (s32[4]{0:T(128)S(1)}, f32[16,512,128]{2,0,1:T(8,128)}, s32[16]{0:T(128)S(1)}, f32[4,512,128]{2,1,0:T(8,128)S(1)}) %tuple.202), branch_computations={%region_14.14_spmd, %region_15.15_spmd} | conditional | flops 2097188 | bytes 35652680 | solution.py:101
  978.2 19.3 %conditional.9 = (f32[1,16,4]{1,2,0:T(4,128)S(1)}) conditional(s32[]{:T(128)} %convert_element_type.37, () %tuple.200, (s32[4]{0:T(128)S(1)}, f32[16,512,128]{2,0,1:T(8,128)}, s32[16]{0:T(128)S(1)}, f32[4,512,128]{2,1,0:T(8,128)S(1)}) %tuple.202), branch_computations={%region_14.14_spmd, %region_15.15_spmd} | conditional | flops 2097188 | bytes 35652680 | solution.py:101
  1006.8 19.3 %conditional.9 = (f32[1,16,4]{1,2,0:T(4,128)S(1)}) conditional(s32[]{:T(128)} %convert_element_type.37, () %tuple.200, (s32[4]{0:T(128)S(1)}, f32[16,512,128]{2,0,1:T(8,128)}, s32[16]{0:T(128)S(1)}, f32[4,512,128]{2,1,0:T(8,128)S(1)}) %tuple.202), branch_computations={%region_14.14_spmd, %region_15.15_spmd} | conditional | flops 2097188 | bytes 35652680 | solution.py:101
  1035.3 19.3 %conditional.9 = (f32[1,16,4]{1,2,0:T(4,128)S(1)}) conditional(s32[]{:T(128)} %convert_element_type.37, () %tuple.200, (s32[4]{0:T(128)S(1)}, f32[16,512,128]{2,0,1:T(8,128)}, s32[16]{0:T(128)S(1)}, f32[4,512,128]{2,1,0:T(8,128)S(1)}) %tuple.202), branch_computations={%region_14.14_spmd, %region_15.15_spmd} | conditional | flops 2097188 | bytes 35652680 | solution.py:101
  1063.9 19.3 %conditional.9 = (f32[1,16,4]{1,2,0:T(4,128)S(1)}) conditional(s32[]{:T(128)} %convert_element_type.37, () %tuple.200, (s32[4]{0:T(128)S(1)}, f32[16,512,128]{2,0,1:T(8,128)}, s32[16]{0:T(128)S(1)}, f32[4,512,128]{2,1,0:T(8,128)S(1)}) %tuple.202), branch_computations={%region_14.14_spmd, %region_15.15_spmd} | conditional | flops 2097188 | bytes 35652680 | solution.py:101
  1092.5 19.3 %conditional.9 = (f32[1,16,4]{1,2,0:T(4,128)S(1)}) conditional(s32[]{:T(128)} %convert_element_type.37, () %tuple.200, (s32[4]{0:T(128)S(1)}, f32[16,512,128]{2,0,1:T(8,128)}, s32[16]{0:T(128)S(1)}, f32[4,512,128]{2,1,0:T(8,128)S(1)}) %tuple.202), branch_computations={%region_14.14_spmd, %region_15.15_spmd} | conditional | flops 2097188 | bytes 35652680 | solution.py:101
  1121.1 19.3 %conditional.9 = (f32[1,16,4]{1,2,0:T(4,128)S(1)}) conditional(s32[]{:T(128)} %convert_element_type.37, () %tuple.200, (s32[4]{0:T(128)S(1)}, f32[16,512,128]{2,0,1:T(8,128)}, s32[16]{0:T(128)S(1)}, f32[4,512,128]{2,1,0:T(8,128)S(1)}) %tuple.202), branch_computations={%region_14.14_spmd, %region_15.15_spmd} | conditional | flops 2097188 | bytes 35652680 | solution.py:101
  1149.7 19.3 %conditional.9 = (f32[1,16,4]{1,2,0:T(4,128)S(1)}) conditional(s32[]{:T(128)} %convert_element_type.37, () %tuple.200, (s32[4]{0:T(128)S(1)}, f32[16,512,128]{2,0,1:T(8,128)}, s32[16]{0:T(128)S(1)}, f32[4,512,128]{2,1,0:T(8,128)S(1)}) %tuple.202), branch_computations={%region_14.14_spmd, %region_15.15_spmd} | conditional | flops 2097188 | bytes 35652680 | solution.py:101
  1178.3 19.3 %conditional.9 = (f32[1,16,4]{1,2,0:T(4,128)S(1)}) conditional(s32[]{:T(128)} %convert_element_type.37, () %tuple.200, (s32[4]{0:T(128)S(1)}, f32[16,512,128]{2,0,1:T(8,128)}, s32[16]{0:T(128)S(1)}, f32[4,512,128]{2,1,0:T(8,128)S(1)}) %tuple.202), branch_computations={%region_14.14_spmd, %region_15.15_spmd} | conditional | flops 2097188 | bytes 35652680 | solution.py:101
  1206.8 19.3 %conditional.9 = (f32[1,16,4]{1,2,0:T(4,128)S(1)}) conditional(s32[]{:T(128)} %convert_element_type.37, () %tuple.200, (s32[4]{0:T(128)S(1)}, f32[16,512,128]{2,0,1:T(8,128)}, s32[16]{0:T(128)S(1)}, f32[4,512,128]{2,1,0:T(8,128)S(1)}) %tuple.202), branch_computations={%region_14.14_spmd, %region_15.15_spmd} | conditional | flops 2097188 | bytes 35652680 | solution.py:101
  1235.4 19.3 %conditional.9 = (f32[1,16,4]{1,2,0:T(4,128)S(1)}) conditional(s32[]{:T(128)} %convert_element_type.37, () %tuple.200, (s32[4]{0:T(128)S(1)}, f32[16,512,128]{2,0,1:T(8,128)}, s32[16]{0:T(128)S(1)}, f32[4,512,128]{2,1,0:T(8,128)S(1)}) %tuple.202), branch_computations={%region_14.14_spmd, %region_15.15_spmd} | conditional | flops 2097188 | bytes 35652680 | solution.py:101
  1254.8 78.3 %all_to_all.10 = f32[32,2,16,2]{2,3,1,0:T(2,128)S(1)} all-to-all(f32[32,2,16,2]{2,3,1,0:T(2,128)S(1)} %fusion.22), channel_id=1, replica_groups=mesh['bl'=32,'bp'=4] {'bl'}, dimensions={0} | all-to-all | bytes 16384 | tf_op jit(solution)/shard_map/all_to_all | solution.py:44
  (984 shorter events, 1104.2 us)
Async XLA Ops:
  0.0 43.9 %copy-start.1 = (s32[1,2]{1,0:T(1,128)S(1)}, s32[1,2]{1,0:T(1,128)}, u32[]{:S(2)}) copy-start(s32[1,2]{1,0:T(1,128)} %param.22) | copy-start | bytes 28
  0.0 45.9 %copy-start = (s32[2,64]{1,0:T(2,128)S(1)}, s32[2,64]{1,0:T(2,128)}, u32[]{:S(2)}) copy-start(s32[2,64]{1,0:T(2,128)} %param.23) | copy-start | bytes 1540
  3.5 30.6 %all-to-all-start = ((f32[4,1,256,512]{3,2,1,0:T(8,128)}), f32[4,1,256,512]{3,2,1,0:T(8,128)}, u32[]{:S(2)}, u32[]{:S(2)}) async-start(f32[4,1,256,512]{3,2,1,0:T(8,128)} %broadcast_in_dim.53), calls=%async_computation | async-start | bytes 4194304 | tf_op jit(solution)/shard_map/all_to_all | solution.py:23
  34.1 123.1 %collective-permute-start = (f32[1,2,512,512]{3,2,1,0:T(8,128)}, f32[1,2,512,512]{3,2,1,0:T(8,128)}, u32[]{:S(2)}, u32[]{:S(2)}) collective-permute-start(f32[1,2,512,512]{3,2,1,0:T(8,128)} %bitcast.30), channel_id=1, source_target_pairs={{0,124},{4,0},{8,4},{12,8},{16,12},{20,16},{24,20},{28,24},{32,28}... | collective-permute-start | bytes 6291464 | tf_op jit(solution)/shard_map/ppermute | solution.py:33
  42.4 114.7 %collective-permute-start.1 = (f32[1,2,512,512]{3,2,1,0:T(8,128)}, f32[1,2,512,512]{3,2,1,0:T(8,128)S(1)}, u32[]{:S(2)}, u32[]{:S(2)}) collective-permute-start(f32[1,2,512,512]{3,2,1,0:T(8,128)} %bitcast.30), channel_id=1, source_target_pairs={{0,120},{4,124},{8,0},{12,4},{16,8},{20,12},{24,16},{28,20},{32,24... | collective-permute-start | bytes 6291464 | tf_op jit(solution)/shard_map/ppermute | solution.py:33
  43.0 114.2 %collective-permute-start.2 = (f32[1,2,512,512]{3,2,1,0:T(8,128)}, f32[1,2,512,512]{3,2,1,0:T(8,128)}, u32[]{:S(2)}, u32[]{:S(2)}) collective-permute-start(f32[1,2,512,512]{3,2,1,0:T(8,128)} %bitcast.30), channel_id=1, source_target_pairs={{0,116},{4,120},{8,124},{12,0},{16,4},{20,8},{24,12},{28,16},{32,2... | collective-permute-start | bytes 6291464 | tf_op jit(solution)/shard_map/ppermute | solution.py:33
  43.7 113.4 %collective-permute-start.3 = (f32[1,2,512,512]{3,2,1,0:T(8,128)}, f32[1,2,512,512]{3,2,1,0:T(8,128)}, u32[]{:S(2)}, u32[]{:S(2)}) collective-permute-start(f32[1,2,512,512]{3,2,1,0:T(8,128)} %bitcast.30), channel_id=1, source_target_pairs={{0,112},{4,116},{8,120},{12,124},{16,0},{20,4},{24,8},{28,12},{32,... | collective-permute-start | bytes 6291464 | tf_op jit(solution)/shard_map/ppermute | solution.py:33
where the time goes:
time: 1340 us; the launch traced here: 1330 us
  local copies, waits for them, and re-layouts  797 us (59%)
  other arithmetic  162 us (12%)
  waiting for transfers between devices  129 us (10%)
  matrix products  106 us (8%)
  blocking collectives  78.3 us (6%)
  loops' own time  44.6 us (3%)
  starting transfers between devices  15.6 us (1%)
    gather x64, local copies, waits for them, and re-layouts, one_matrix(): lax.dynamic_slice_in_dim(matrix, row_start, window, 0)  309 us
    gather x480, local copies, waits for them, and re-layouts  285 us
    cond x32, other arithmetic  149 us
    cond x34, local copies, waits for them, and re-layouts  140 us
    dot_general x34, matrix products, project_turned(): jnp.einsum('apq,aqc->acp', kernels, window_rows, precision=highest, prefe...  106 us
    ppermute x4, waiting for transfers between devices, passed_along(): return lax.ppermute(value, axis, pairs)  104 us
    all_to_all x1, blocking collectives, sent_and_summed(): tiles = lax.all_to_all(split_up(x, dim, length), axis, 0, 0, tiled=True)  78.3 us
    another operation x2, loops' own time, body(): block_sums = lax.map(stepper, jnp.arange(block_count, dtype=jnp.int32))  40.8 us
  transfers between devices with their start and end apart: 5, of which 2 were waited for; matrix products, arithmetic and copies ran while one was open for 1% of the time, Pallas kernels for 0%

commit v1 on v0

v1 whole, which is shorter than its diff:
```python
import functools

import jax
import jax.numpy as jnp
from jax import lax
from jax.experimental import pallas as pl
from jax.experimental.pallas import tpu as pltpu
from jax.sharding import PartitionSpec as P

MESH = pl.DeviceIdType.MESH
F32 = jnp.float32
BF16 = jnp.bfloat16

GROUPS = 32
REACH = 4
PANEL = 512
ROWS = 256
BANDS = 64
WINDOW = 128
CLASSES = 4
CHUNKS = 2
CHUNK_ROWS = ROWS // CHUNKS
SCALE = 1.0 / (4 * GROUPS * WINDOW)


def split(x):
    hi = x.astype(BF16)
    return hi, (x - hi.astype(F32)).astype(BF16)


def mm(a, b):
    return jnp.dot(a, b, preferred_element_type=F32)


def dot3(a, b):
    return mm(a[0], b[0]) + (mm(a[0], b[1]) + mm(a[1], b[0]))


def iota(shape, dim):
    return lax.broadcasted_iota(jnp.int32, shape, dim)


def down(row, count):
    return jnp.transpose(jnp.broadcast_to(row, (128, count)))


def body_kernel(
    inv_ref, mask_ref, partner_ref, start_ref, out_ref,
    own_raw, got, got_mask, toep_hi, toep_lo, edge_hi, edge_lo, win, decay_hi, decay_lo,
    decay_t_hi, decay_t_lo, edge_t_hi, edge_t_lo, win_t, panel_hi, panel_lo, filt, filt_edge,
    outer, outer_decay, mixed, gram, total, mirror,
    sum_x, got_x, sum_y, got_y, sum_z, got_z,
    send_sem, recv_sem, mask_send, mask_recv, sib_sem, own_sem, x_sem, y_sem, z_sem,
):
    me = lax.axis_index("bl")
    part = lax.axis_index("bp")
    half = part // 2
    core = part % 2
    pos_x = me % 4
    pos_y = (me // 4) % 4
    pos_z = me // 16
    first = pl.multiple_of(core * ROWS, ROWS)
    col0 = pl.multiple_of(half * PANEL, PANEL)
    sibling = (me, part + 1 - 2 * core)

    def target(d):
        return ((me + GROUPS - d) % GROUPS, part)

    def source(d):
        return ((me + d) % GROUPS, part)

    def x_peer(e):
        return (me - pos_x + (pos_x + e) % 4, part)

    def y_peer(e):
        return (me - 4 * pos_y + 4 * ((pos_y + e) % 4), part)

    spot = pos_z * 4 + part

    def z_peer(e):
        g = (spot + e) % 8
        return (me % 16 + 16 * (g // 4), g % 4)

    peers = (
        [target(d) for d in range(1, REACH + 1)]
        + [source(d) for d in range(1, REACH + 1)]
        + [x_peer(e) for e in range(1, 4)]
        + [y_peer(e) for e in range(1, 4)]
        + [z_peer(e) for e in range(1, 8)]
    )
    barrier = pltpu.get_barrier_semaphore()
    for peer in peers:
        pl.semaphore_signal(barrier, inc=1, device_id=peer, device_id_type=MESH)

    own_rows = own_raw.at[pl.ds(first, ROWS)]
    own_copy = pltpu.make_async_copy(inv_ref.at[0, :, pl.ds(col0, PANEL)], own_rows, own_sem)
    own_copy.start()
    pl.semaphore_wait(barrier, len(peers))

    sib_copy = pltpu.make_async_remote_copy(
        src_ref=inv_ref.at[0, :, pl.ds(col0, PANEL)], dst_ref=own_rows,
        send_sem=sib_sem.at[0], recv_sem=sib_sem.at[1], device_id=sibling, device_id_type=MESH,
    )
    sib_copy.start()
    mask_copies = []
    for d in range(REACH):
        copy = pltpu.make_async_remote_copy(
            src_ref=mask_ref, dst_ref=got_mask.at[d],
            send_sem=mask_send.at[d], recv_sem=mask_recv.at[d],
            device_id=target(d + 1), device_id_type=MESH,
        )
        copy.start()
        mask_copies.append(copy)
    copies = {}
    for k in range(CHUNKS):
        for d in range(REACH):
            copy = pltpu.make_async_remote_copy(
                src_ref=inv_ref.at[0, pl.ds(k * CHUNK_ROWS, CHUNK_ROWS), pl.ds(col0, PANEL)],
                dst_ref=got.at[d, pl.ds(k * CHUNK_ROWS, CHUNK_ROWS)],
                send_sem=send_sem.at[d, k], recv_sem=recv_sem.at[d, k],
                device_id=target(d + 1), device_id_type=MESH,
            )
            copy.start()
            copies[d, k] = copy

    starts = start_ref[pl.ds(half, 1), :]
    starts2 = jnp.concatenate([starts, starts], axis=1)
    lane = iota((1, 2 * BANDS), 1)
    lane_class = lane % CLASSES
    rate = 1.0 / (1 + lane_class).astype(F32)
    is_left = lane < BANDS
    for r0 in range(0, PANEL, 128):
        pos = iota((128, 2 * BANDS), 0) + r0
        from_start = pos - starts2
        to_end = starts2 + (WINDOW - 1) - pos
        inside = (from_start >= 0) & (to_end >= 0)
        gap = jnp.where(is_left, -from_start, -to_end)
        edge = jnp.where(gap > 0, jnp.exp(-jnp.abs(gap).astype(F32) * rate), 0.0)
        edge_hi[r0 : r0 + 128, :], edge_lo[r0 : r0 + 128, :] = split(edge)
        decay = jnp.where(inside, jnp.exp(-jnp.abs(gap).astype(F32) * rate), 0.0)
        decay_hi[r0 : r0 + 128, :], decay_lo[r0 : r0 + 128, :] = split(decay)
        for l in range(CLASSES):
            one = jnp.where(inside & (lane_class == l), 1.0, 0.0)[:, :BANDS]
            win[l * PANEL + r0 : l * PANEL + r0 + 128, :] = one.astype(BF16)
    starts_t = down(starts2.astype(F32), 2 * BANDS).astype(jnp.int32)
    sub = iota((2 * BANDS, 128), 0)
    sub_class = sub % CLASSES
    rate_t = 1.0 / (1 + sub_class).astype(F32)
    is_left_t = sub < BANDS
    for r0 in range(0, PANEL, 128):
        pos = iota((2 * BANDS, 128), 1) + r0
        from_start = pos - starts_t
        to_end = starts_t + (WINDOW - 1) - pos
        inside = (from_start >= 0) & (to_end >= 0)
        gap = jnp.where(is_left_t, -from_start, -to_end)
        weight = jnp.exp(-jnp.abs(gap).astype(F32) * rate_t)
        edge_t_hi[:, r0 : r0 + 128], edge_t_lo[:, r0 : r0 + 128] = split(
            jnp.where(gap > 0, weight, 0.0)
        )
        decay_t_hi[:, r0 : r0 + 128], decay_t_lo[:, r0 : r0 + 128] = split(
            jnp.where(inside, weight, 0.0)
        )
        for l in range(CLASSES):
            one = jnp.where(inside & (sub_class == l), 1.0, 0.0)[:BANDS, :]
            win_t[l, :, r0 : r0 + 128] = one.astype(BF16)

    def fill(block, carry):
        r0 = pl.multiple_of(block * 128, 128)
        dist = jnp.abs(iota((128, PANEL), 0) + r0 - iota((128, PANEL), 1)).astype(F32)
        for l in range(CLASSES):
            hi, lo = split(jnp.exp(dist * (-1.0 / (1 + l))))
            toep_hi[pl.ds(r0, 128), l * PANEL : (l + 1) * PANEL] = hi
            toep_lo[pl.ds(r0, 128), l * PANEL : (l + 1) * PANEL] = lo
        return carry

    lax.fori_loop(0, PANEL // 128, fill, 0)

    own_copy.wait()
    sib_copy.wait()
    cols = mask_ref[:, pl.ds(col0, PANEL)].astype(F32)
    for r0 in range(0, PANEL, 128):
        marks = down(cols[:, r0 : r0 + 128], 128)
        for c0 in range(0, PANEL, 128):
            block = own_raw[r0 : r0 + 128, c0 : c0 + 128] * marks * cols[:, c0 : c0 + 128]
            panel_hi[r0 : r0 + 128, c0 : c0 + 128], panel_lo[r0 : r0 + 128, c0 : c0 + 128] = split(
                block
            )
    panel = (panel_hi[...], panel_lo[...])
    decays = (decay_hi[...], decay_lo[...])
    for l in range(CLASSES):
        rows = (
            toep_hi[pl.ds(first, ROWS), l * PANEL : (l + 1) * PANEL],
            toep_lo[pl.ds(first, ROWS), l * PANEL : (l + 1) * PANEL],
        )
        out = dot3(rows, panel)
        filt[l] = out
        filt_edge[l] = dot3(split(out), decays)
    outer[...] = dot3((edge_t_hi[...], edge_t_lo[...]), panel)
    outer_decay[...] = dot3(split(outer[...]), decays)

    for d in range(REACH):
        mask_copies[d].wait()
    total[...] = jnp.zeros_like(total)
    gram[...] = jnp.zeros_like(gram)
    mirror[...] = jnp.zeros_like(mirror)
    weights = []
    for d in range(REACH):
        wanted = (me + d + 1) % GROUPS
        weight = 0.0
        for slot in range(2):
            weight = weight + jnp.where(partner_ref[0, slot] == wanted, 1.0, 0.0)
        weights.append(weight)
    for k in range(CHUNKS):
        y0 = k * CHUNK_ROWS
        for d in range(REACH):
            copies[d, k].wait_recv()
        blocks = [0.0] * (PANEL // 128)
        for d in range(REACH):
            row_marks = got_mask[d, :, pl.ds(pl.multiple_of(col0 + first + y0, 128), CHUNK_ROWS)]
            marks = down(row_marks.astype(F32) * weights[d], CHUNK_ROWS)
            cols = got_mask[d, :, pl.ds(col0, PANEL)].astype(F32)
            for c in range(PANEL // 128):
                span = slice(c * 128, c * 128 + 128)
                blocks[c] = blocks[c] + got[d, y0 : y0 + CHUNK_ROWS, span] * marks * cols[:, span]
        rows = split(jnp.concatenate(blocks, axis=1))
        here = pl.ds(pl.multiple_of(first + y0, 128), CHUNK_ROWS)
        decay_t = (decay_t_hi[:, here], decay_t_lo[:, here])
        edges = dot3(rows, (edge_hi[...], edge_lo[...]))
        mirror[...] += dot3(decay_t, split(edges))
        for l in range(CLASSES):
            span = slice(l * PANEL, (l + 1) * PANEL)
            out = dot3(rows, (toep_hi[:, span], toep_lo[:, span]))
            mixed[:, span] = out
            gram[:, span] += dot3(decay_t, split(out))
        acc = jnp.zeros((BANDS, BANDS), F32)
        for lb in range(CLASSES):
            rim = edges * filt_edge[lb, y0 : y0 + CHUNK_ROWS, :]
            sums = -(rim[:, :BANDS] + rim[:, BANDS:])
            for la in range(CLASSES):
                span = slice(la * PANEL, (la + 1) * PANEL)
                hi, lo = split(mixed[:, span] * filt[lb, y0 : y0 + CHUNK_ROWS, :])
                sums = sums + (mm(hi, win[span, :]) + mm(lo, win[span, :]))
            hi, lo = split(sums)
            acc = acc + (mm(win_t[lb, :, here], hi) + mm(win_t[lb, :, here], lo))
        total[...] += acc
    cross = jnp.zeros((2 * BANDS, BANDS), F32)
    for la in range(CLASSES):
        span = slice(la * PANEL, (la + 1) * PANEL)
        hi, lo = split(gram[:, span] * outer[...])
        cross = cross + (mm(hi, win[span, :]) + mm(lo, win[span, :]))
    four = mirror[...] * outer_decay[...]
    fisher = total[...] - cross[:BANDS] - cross[BANDS:]
    fisher = fisher + (four[:BANDS, :BANDS] + four[:BANDS, BANDS:])
    fisher = fisher + (four[BANDS:, :BANDS] + four[BANDS:, BANDS:])
    fisher = fisher * SCALE

    row = iota((BANDS // 2, BANDS), 0)
    owner = (row % 2) * 16 + ((row // 2) % 4) * 4 + row // 8
    col = iota((BANDS // 2, BANDS), 1)
    parts3 = []
    rest = fisher
    for _ in range(3):
        piece = rest.astype(BF16)
        parts3.append(piece)
        rest = rest - piece.astype(F32)
    turned = []
    for side in range(2):
        pick = jnp.where(col == 2 * owner + side, 1.0, 0.0).astype(BF16)
        turned.append(mm(pick, parts3[0]) + mm(pick, parts3[1]) + mm(pick, parts3[2]))
    placed = jnp.concatenate(turned, axis=1)
    for x in range(4):
        sum_x[x] = placed[8 * x : 8 * x + 8]

    x_copies = []
    for e in range(1, 4):
        copy = pltpu.make_async_remote_copy(
            src_ref=sum_x.at[(pos_x + e) % 4], dst_ref=got_x.at[e - 1],
            send_sem=x_sem.at[0, e - 1], recv_sem=x_sem.at[1, e - 1],
            device_id=x_peer(e), device_id_type=MESH,
        )
        copy.start()
        x_copies.append(copy)
    tile = sum_x[pos_x]
    for e in range(3):
        x_copies[e].wait_recv()
        tile = tile + got_x[e]
    sum_y[...] = tile
    y_copies = []
    for e in range(1, 4):
        copy = pltpu.make_async_remote_copy(
            src_ref=sum_y, dst_ref=got_y.at[e - 1],
            send_sem=y_sem.at[0, e - 1], recv_sem=y_sem.at[1, e - 1],
            device_id=y_peer(e), device_id_type=MESH,
        )
        copy.start()
        y_copies.append(copy)
    for e in range(3):
        y_copies[e].wait_recv()
        tile = tile + got_y[e]
    sum_z[...] = tile
    z_copies = []
    for e in range(1, 8):
        copy = pltpu.make_async_remote_copy(
            src_ref=sum_z, dst_ref=got_z.at[e - 1],
            send_sem=z_sem.at[0, e - 1], recv_sem=z_sem.at[1, e - 1],
            device_id=z_peer(e), device_id_type=MESH,
        )
        copy.start()
        z_copies.append(copy)
    halves = [jnp.where(half == h, tile, 0.0) for h in range(2)]
    for e in range(7):
        z_copies[e].wait_recv()
        from_half = ((spot + 7 - e) % 8 % 4) // 2
        for h in range(2):
            halves[h] = halves[h] + jnp.where(from_half == h, got_z[e], 0.0)
    my_row = pos_y * 2 + pos_z
    lanes = iota((16, 128), 1)
    for h in range(2):
        line = jnp.sum(jnp.where(iota((8, 128), 0) == my_row, halves[h], 0.0), axis=0, keepdims=True)
        line = jnp.broadcast_to(line, (16, 128))
        band = 16 * part + iota((16, 128), 0)
        for side in range(2):
            one = jnp.where(lanes == band + side * BANDS, line, 0.0)
            out_ref[h, :, side : side + 1] = jnp.sum(one, axis=1, keepdims=True)

    for copy in list(copies.values()) + x_copies + y_copies + z_copies:
        copy.wait_send()


def body(inverse_cov, channel_keep_mask, partner_ids, band_starts):
    vmem = pltpu.VMEM
    dma = pltpu.SemaphoreType.DMA
    return pl.pallas_call(
        body_kernel,
        out_shape=jax.ShapeDtypeStruct((2, 16, 2), F32),
        in_specs=[
            pl.BlockSpec(memory_space=pl.ANY),
            pl.BlockSpec(memory_space=pltpu.VMEM),
            pl.BlockSpec(memory_space=pltpu.SMEM),
            pl.BlockSpec(memory_space=pltpu.VMEM),
        ],
        out_specs=pl.BlockSpec(memory_space=pltpu.VMEM),
        scratch_shapes=[
            vmem((PANEL, PANEL), F32),
            vmem((REACH, ROWS, PANEL), F32),
            vmem((REACH, 1, 2 * PANEL), jnp.int32),
            vmem((PANEL, CLASSES * PANEL), BF16),
            vmem((PANEL, CLASSES * PANEL), BF16),
            vmem((PANEL, 2 * BANDS), BF16),
            vmem((PANEL, 2 * BANDS), BF16),
            vmem((CLASSES * PANEL, BANDS), BF16),
            vmem((PANEL, 2 * BANDS), BF16),
            vmem((PANEL, 2 * BANDS), BF16),
            vmem((2 * BANDS, PANEL), BF16),
            vmem((2 * BANDS, PANEL), BF16),
            vmem((2 * BANDS, PANEL), BF16),
            vmem((2 * BANDS, PANEL), BF16),
            vmem((CLASSES, BANDS, PANEL), BF16),
            vmem((PANEL, PANEL), BF16),
            vmem((PANEL, PANEL), BF16),
            vmem((CLASSES, ROWS, PANEL), F32),
            vmem((CLASSES, ROWS, 2 * BANDS), F32),
            vmem((2 * BANDS, PANEL), F32),
            vmem((2 * BANDS, 2 * BANDS), F32),
            vmem((CHUNK_ROWS, CLASSES * PANEL), F32),
            vmem((2 * BANDS, CLASSES * PANEL), F32),
            vmem((BANDS, BANDS), F32),
            vmem((2 * BANDS, 2 * BANDS), F32),
            vmem((4, 8, 128), F32),
            vmem((3, 8, 128), F32),
            vmem((8, 128), F32),
            vmem((3, 8, 128), F32),
            vmem((8, 128), F32),
            vmem((7, 8, 128), F32),
            dma((REACH, CHUNKS)),
            dma((REACH, CHUNKS)),
            dma((REACH,)),
            dma((REACH,)),
            dma((2,)),
            dma,
            dma((2, 3)),
            dma((2, 3)),
            dma((2, 7)),
        ],
        compiler_params=pltpu.CompilerParams(
            collective_id=0, has_side_effects=True, vmem_limit_bytes=48 * 1024 * 1024
        ),
    )(inverse_cov, channel_keep_mask, partner_ids, band_starts)


def solution(mesh):
    placed = (P("bl", "bp", None), P("bl", None), P("bl", None), P())
    return jax.shard_map(
        body, mesh=mesh, in_specs=placed, out_specs=P(None, "bp", "bl"), check_vma=False
    )
```

time: 1340 us -> 77 us (0.06)
  local copies, waits for them, and re-layouts: 797 us -> 3.9 us
  other arithmetic: 162 us -> 0 us
  waiting for transfers between devices: 129 us -> 0 us
  matrix products: 106 us -> 0 us
  blocking collectives: 78.3 us -> 0 us
  Pallas kernels: 0 us -> 72.9 us
  loops' own time: 44.6 us -> 0 us
  starting transfers between devices: 15.6 us -> 0 us
    gather x544 -> x0, local copies, waits for them, and re-layouts: 594 us -> none  [the longest x64 309 us: one_matrix(): lax.dynamic_slice_in_dim(matrix, row_start, window, 0)]
    cond x32 -> x0, other arithmetic: 149 us -> none
    cond x34 -> x0, local copies, waits for them, and re-layouts: 140 us -> none
    dot_general x34 -> x0, matrix products: 106 us -> none  [project_turned(): jnp.einsum('apq,aqc->acp', kernels, window_rows, precision=highest, prefe...]
    ppermute x4 -> x0, waiting for transfers between devices: 104 us -> none  [passed_along(): return lax.ppermute(value, axis, pairs)]
    all_to_all x1 -> x0, blocking collectives: 78.3 us -> none  [sent_and_summed(): tiles = lax.all_to_all(split_up(x, dim, length), axis, 0, 0, tiled=True)]
    pallas_call x0 -> x1, Pallas kernels: none -> 72.9 us  [body(): pl.pallas_call(body_kernel, out_shape=jax.ShapeDtypeStruct((2, 16, 2), F3...]
    another operation x70 -> x0, loops' own time: 44.6 us -> none  [the longest x2 40.8 us: body(): block_sums = lax.map(stepper, jnp.arange(block_count, dtype=jnp.int32))]
  transfers between devices with their start and end apart: 5 -> 0, of which waited for: 2 -> 0; matrix products, arithmetic and copies ran while one was open for 1% -> 0% of each run, Pallas kernels for 0% -> 0%
where the time goes in v1:
time: 77 us; the launch traced here: 76.8 us
  Pallas kernels  72.9 us (95%)
  local copies, waits for them, and re-layouts  3.9 us (5%)
    pallas_call x1, Pallas kernels, body(): pl.pallas_call(body_kernel, out_shape=jax.ShapeDtypeStruct((2, 16, 2), F3...  72.9 us
    unnamed x8, local copies, waits for them, and re-layouts  3.24 us

profile of v1, /device:TPU:1, one launch (start us, length us, event | category | flops | bytes accessed | tf_op | source)
XLA Modules:
  0.0 76.8 jit_solution(3609164608183834372)
XLA Ops:
  0.0 0.0 copy-start
  0.0 1.2 %copy-done = f32[1,256,1024]{2,1,0:T(8,128)S(1)} copy-done((f32[1,256,1024]{2,1,0:T(8,128)S(1)}, f32[1,256,1024]{2,1,0:T(8,128)}, u32[]{:S(2)}) %copy-start) | copy-done | bytes 1048600
  1.2 0.0 copy-start.1
  1.2 0.7 copy-done.1
  1.9 0.0 copy-start.2
  1.9 0.7 copy-done.2
  2.6 0.0 copy-start.3
  2.6 0.7 copy-done.3
  3.2 72.9 %shard_map.46 = f32[2,16,2]{2,1,0:T(8,128)S(1)} custom-call(f32[1,256,1024]{2,1,0:T(8,128)S(1)} %copy-done, s32[1,1024]{1,0:T(1,128)S(1)} %copy-done.1, s32[1,2]{1,0:T(1,128)S(1)} %copy-done.3, s32[2,64]{1,0:T(2,128)S(1)} %copy-done.2), custom_call_target="tpu_custom_call" | custom-call | tf_op jit(solution)/shard_map/pallas_call | solution.py:333
  76.2 0.7 copy.5
Async XLA Ops:
  0.0 1.2 %copy-start = (f32[1,256,1024]{2,1,0:T(8,128)S(1)}, f32[1,256,1024]{2,1,0:T(8,128)}, u32[]{:S(2)}) copy-start(f32[1,256,1024]{2,1,0:T(8,128)} %inv_ref.1) | copy-start | bytes 3145732
  1.2 0.7 copy-start.1
  1.9 0.7 copy-start.2
  2.6 0.7 copy-start.3

commit v2 on v1

--- a/solution.py
+++ b/solution.py
@@ -13,13 +13,14 @@
 
 GROUPS = 32
 REACH = 4
+SENDS = (-1, 2, -3, 4)
+BLOCK = 128
+GROUPS_OF_BLOCKS = ((0, 2), (2, 2), (4, 1))
 PANEL = 512
 ROWS = 256
 BANDS = 64
 WINDOW = 128
 CLASSES = 4
-CHUNKS = 2
-CHUNK_ROWS = ROWS // CHUNKS
 SCALE = 1.0 / (4 * GROUPS * WINDOW)
 
 
@@ -45,12 +46,14 @@
 
 
 def body_kernel(
-    inv_ref, mask_ref, partner_ref, start_ref, out_ref,
-    own_raw, got, got_mask, toep_hi, toep_lo, edge_hi, edge_lo, win, decay_hi, decay_lo,
+    inv_ref, mask_hbm, partner_hbm, start_hbm, out_ref,
+    mask_ref, partner_ref, start_ref, own_raw, own_pack, got, got_mask, got_partner, row_marks,
+    far_sum, got_far, rows_hi, rows_lo,
+    toep_hi, toep_lo, edge_hi, edge_lo, win, decay_hi, decay_lo,
     decay_t_hi, decay_t_lo, edge_t_hi, edge_t_lo, win_t, panel_hi, panel_lo, filt, filt_edge,
     outer, outer_decay, mixed, gram, total, mirror,
     sum_x, got_x, sum_y, got_y, sum_z, got_z,
-    send_sem, recv_sem, mask_send, mask_recv, sib_sem, own_sem, x_sem, y_sem, z_sem,
+    send_sem, recv_sem, mask_sem, partner_sem, sib_sem, far_sem, own_sem, x_sem, y_sem, z_sem,
 ):
     me = lax.axis_index("bl")
     part = lax.axis_index("bp")
@@ -63,11 +66,23 @@
     col0 = pl.multiple_of(half * PANEL, PANEL)
     sibling = (me, part + 1 - 2 * core)
 
+    def by_core(zero, one):
+        return core * (one - zero) + zero
+
     def target(d):
-        return ((me + GROUPS - d) % GROUPS, part)
+        return ((me + GROUPS + SENDS[d]) % GROUPS, part)
 
     def source(d):
-        return ((me + d) % GROUPS, part)
+        return ((me + GROUPS - SENDS[d]) % GROUPS, part)
+
+    near = [2 * core, 2 * core + 1]
+    far = [by_core(2 + r, 1 - r) for r in range(2)]
+    missing = [by_core(3 - r, r) for r in range(2)]
+    missing_slot = [by_core(1 - r, r) for r in range(2)]
+    pack = [(0, far[0]), (1, far[1]), (0, near[0]), (0, near[1]), (1, near[1])]
+
+    def lanes_of(block):
+        return pl.ds(pl.multiple_of(col0 + BLOCK * block, BLOCK), BLOCK)
 
     def x_peer(e):
         return (me - pos_x + (pos_x + e) % 4, part)
@@ -82,8 +97,8 @@
         return (me % 16 + 16 * (g // 4), g % 4)
 
     peers = (
-        [target(d) for d in range(1, REACH + 1)]
-        + [source(d) for d in range(1, REACH + 1)]
+        [target(d) for d in range(REACH)]
+        + [source(d) for d in range(REACH)]
         + [x_peer(e) for e in range(1, 4)]
         + [y_peer(e) for e in range(1, 4)]
         + [z_peer(e) for e in range(1, 8)]
@@ -92,36 +107,52 @@
     for peer in peers:
         pl.semaphore_signal(barrier, inc=1, device_id=peer, device_id_type=MESH)
 
+    locals_ = [
+        pltpu.make_async_copy(
+            inv_ref.at[0, BLOCK * r : BLOCK * (r + 1), lanes_of(c)], own_pack.at[p], own_sem.at[p]
+        )
+        for p, (r, c) in enumerate(pack)
+    ]
     own_rows = own_raw.at[pl.ds(first, ROWS)]
-    own_copy = pltpu.make_async_copy(inv_ref.at[0, :, pl.ds(col0, PANEL)], own_rows, own_sem)
-    own_copy.start()
+    locals_.append(
+        pltpu.make_async_copy(inv_ref.at[0, :, pl.ds(col0, PANEL)], own_rows, own_sem.at[5])
+    )
+    locals_.append(pltpu.make_async_copy(mask_hbm, mask_ref, own_sem.at[6]))
+    locals_.append(pltpu.make_async_copy(partner_hbm, partner_ref, own_sem.at[7]))
+    locals_.append(pltpu.make_async_copy(start_hbm, start_ref, own_sem.at[8]))
+    for copy in locals_:
+        copy.start()
+    for copy in locals_:
+        copy.wait()
     pl.semaphore_wait(barrier, len(peers))
 
     sib_copy = pltpu.make_async_remote_copy(
-        src_ref=inv_ref.at[0, :, pl.ds(col0, PANEL)], dst_ref=own_rows,
+        src_ref=own_rows, dst_ref=own_rows,
         send_sem=sib_sem.at[0], recv_sem=sib_sem.at[1], device_id=sibling, device_id_type=MESH,
     )
     sib_copy.start()
     mask_copies = []
     for d in range(REACH):
-        copy = pltpu.make_async_remote_copy(
-            src_ref=mask_ref, dst_ref=got_mask.at[d],
-            send_sem=mask_send.at[d], recv_sem=mask_recv.at[d],
-            device_id=target(d + 1), device_id_type=MESH,
-        )
-        copy.start()
-        mask_copies.append(copy)
+        pairs = [(mask_ref, got_mask, mask_sem)]
+        if SENDS[d] > 0:
+            pairs.append((partner_ref, got_partner, partner_sem))
+        for src, dst, sem in pairs:
+            copy = pltpu.make_async_remote_copy(
+                src_ref=src, dst_ref=dst.at[d], send_sem=sem.at[0, d], recv_sem=sem.at[1, d],
+                device_id=target(d), device_id_type=MESH,
+            )
+            copy.start()
+            mask_copies.append(copy)
     copies = {}
-    for k in range(CHUNKS):
+    for g, (p, count) in enumerate(GROUPS_OF_BLOCKS):
         for d in range(REACH):
             copy = pltpu.make_async_remote_copy(
-                src_ref=inv_ref.at[0, pl.ds(k * CHUNK_ROWS, CHUNK_ROWS), pl.ds(col0, PANEL)],
-                dst_ref=got.at[d, pl.ds(k * CHUNK_ROWS, CHUNK_ROWS)],
-                send_sem=send_sem.at[d, k], recv_sem=recv_sem.at[d, k],
-                device_id=target(d + 1), device_id_type=MESH,
+                src_ref=own_pack.at[pl.ds(p, count)], dst_ref=got.at[d, pl.ds(p, count)],
+                send_sem=send_sem.at[d, g], recv_sem=recv_sem.at[d, g],
+                device_id=target(d), device_id_type=MESH,
             )
             copy.start()
-            copies[d, k] = copy
+            copies[d, g] = copy
 
     starts = start_ref[pl.ds(half, 1), :]
     starts2 = jnp.concatenate([starts, starts], axis=1)
@@ -175,7 +206,6 @@
 
     lax.fori_loop(0, PANEL // 128, fill, 0)
 
-    own_copy.wait()
     sib_copy.wait()
     cols = mask_ref[:, pl.ds(col0, PANEL)].astype(F32)
     for r0 in range(0, PANEL, 128):
@@ -198,32 +228,62 @@
     outer[...] = dot3((edge_t_hi[...], edge_t_lo[...]), panel)
     outer_decay[...] = dot3(split(outer[...]), decays)
 
-    for d in range(REACH):
-        mask_copies[d].wait()
+    for copy in mask_copies:
+        copy.wait()
     total[...] = jnp.zeros_like(total)
     gram[...] = jnp.zeros_like(gram)
     mirror[...] = jnp.zeros_like(mirror)
-    weights = []
     for d in range(REACH):
-        wanted = (me + d + 1) % GROUPS
-        weight = 0.0
-        for slot in range(2):
-            weight = weight + jnp.where(partner_ref[0, slot] == wanted, 1.0, 0.0)
-        weights.append(weight)
-    for k in range(CHUNKS):
-        y0 = k * CHUNK_ROWS
+        if SENDS[d] < 0:
+            hits = jnp.where(partner_ref[...] == source(d)[0], 1.0, 0.0)
+        else:
+            hits = jnp.where(got_partner[d] == me, 1.0, 0.0)
+        weight = hits[:, 0:1] + hits[:, 1:2]
+        for r in range(2):
+            marks = got_mask[d, :, lanes_of(near[r])].astype(F32) * weight
+            row_marks[d, r] = down(marks, BLOCK)
+
+    def summed(p):
+        r, c = pack[p]
+        out = 0.0
         for d in range(REACH):
-            copies[d, k].wait_recv()
-        blocks = [0.0] * (PANEL // 128)
+            cols = got_mask[d, :, lanes_of(c)].astype(F32)
+            out = out + got[d, p] * row_marks[d, r] * cols
+        return out
+
+    def put(block, value):
+        hi, lo = split(value)
+        spot = pl.ds(pl.multiple_of(BLOCK * block, BLOCK), BLOCK)
+        rows_hi[:, spot] = hi
+        rows_lo[:, spot] = lo
+
+    far_copy = pltpu.make_async_remote_copy(
+        src_ref=far_sum, dst_ref=got_far,
+        send_sem=far_sem.at[0], recv_sem=far_sem.at[1], device_id=sibling, device_id_type=MESH,
+    )
+    for d in range(REACH):
+        copies[d, 0].wait_recv()
+    for r in range(2):
+        far_sum[r] = summed(r)
+    far_copy.start()
+    for k in range(2):
+        y0 = k * BLOCK
         for d in range(REACH):
-            row_marks = got_mask[d, :, pl.ds(pl.multiple_of(col0 + first + y0, 128), CHUNK_ROWS)]
-            marks = down(row_marks.astype(F32) * weights[d], CHUNK_ROWS)
-            cols = got_mask[d, :, pl.ds(col0, PANEL)].astype(F32)
-            for c in range(PANEL // 128):
-                span = slice(c * 128, c * 128 + 128)
-                blocks[c] = blocks[c] + got[d, y0 : y0 + CHUNK_ROWS, span] * marks * cols[:, span]
-        rows = split(jnp.concatenate(blocks, axis=1))
-        here = pl.ds(pl.multiple_of(first + y0, 128), CHUNK_ROWS)
+            copies[d, k + 1].wait_recv()
+        if k == 0:
+            far_copy.wait_recv()
+        put(far[k], far_sum[k])
+        put(missing[k], jnp.transpose(got_far[missing_slot[k]]))
+        if k == 0:
+            put(near[0], summed(2))
+            corner = summed(3)
+            put(near[1], corner)
+            row_marks[0, 0] = jnp.transpose(corner)
+        else:
+            put(near[0], row_marks[0, 0])
+            put(near[1], summed(4))
+        rows = (rows_hi[...], rows_lo[...])
+        here = pl.ds(pl.multiple_of(first + y0, BLOCK), BLOCK)
         decay_t = (decay_t_hi[:, here], decay_t_lo[:, here])
         edges = dot3(rows, (edge_hi[...], edge_lo[...]))
         mirror[...] += dot3(decay_t, split(edges))
@@ -234,11 +294,11 @@
             gram[:, span] += dot3(decay_t, split(out))
         acc = jnp.zeros((BANDS, BANDS), F32)
         for lb in range(CLASSES):
-            rim = edges * filt_edge[lb, y0 : y0 + CHUNK_ROWS, :]
+            rim = edges * filt_edge[lb, y0 : y0 + BLOCK, :]
             sums = -(rim[:, :BANDS] + rim[:, BANDS:])
-            for la in range(CLASSES):
+            for la in range(lb + 1):
                 span = slice(la * PANEL, (la + 1) * PANEL)
-                hi, lo = split(mixed[:, span] * filt[lb, y0 : y0 + CHUNK_ROWS, :])
+                hi, lo = split(mixed[:, span] * filt[lb, y0 : y0 + BLOCK, :])
                 sums = sums + (mm(hi, win[span, :]) + mm(lo, win[span, :]))
             hi, lo = split(sums)
             acc = acc + (mm(win_t[lb, :, here], hi) + mm(win_t[lb, :, here], lo))
@@ -252,7 +312,12 @@
     fisher = total[...] - cross[:BANDS] - cross[BANDS:]
     fisher = fisher + (four[:BANDS, :BANDS] + four[:BANDS, BANDS:])
     fisher = fisher + (four[BANDS:, :BANDS] + four[BANDS:, BANDS:])
-    fisher = fisher * SCALE
+    row_class = iota((BANDS, BANDS), 0) % CLASSES
+    col_class = iota((BANDS, BANDS), 1) % CLASSES
+    kept = jnp.where(col_class <= row_class, fisher * SCALE, 0.0)
+    wide = jnp.concatenate([kept, jnp.zeros_like(kept)], axis=1)
+    turned_over = jnp.transpose(jnp.concatenate([wide, jnp.zeros_like(wide)], axis=0))
+    fisher = kept + jnp.where(col_class > row_class, turned_over[:BANDS, :BANDS], 0.0)
 
     row = iota((BANDS // 2, BANDS), 0)
     owner = (row % 2) * 16 + ((row // 2) % 4) * 4 + row // 8
@@ -323,7 +388,7 @@
             one = jnp.where(lanes == band + side * BANDS, line, 0.0)
             out_ref[h, :, side : side + 1] = jnp.sum(one, axis=1, keepdims=True)
 
-    for copy in list(copies.values()) + x_copies + y_copies + z_copies:
+    for copy in list(copies.values()) + [far_copy] + x_copies + y_copies + z_copies:
         copy.wait_send()
 
 
@@ -334,16 +399,26 @@
         body_kernel,
         out_shape=jax.ShapeDtypeStruct((2, 16, 2), F32),
         in_specs=[
-            pl.BlockSpec(memory_space=pl.ANY),
-            pl.BlockSpec(memory_space=pltpu.VMEM),
-            pl.BlockSpec(memory_space=pltpu.SMEM),
-            pl.BlockSpec(memory_space=pltpu.VMEM),
+            pl.BlockSpec(memory_space=pltpu.HBM),
+            pl.BlockSpec(memory_space=pltpu.HBM),
+            pl.BlockSpec(memory_space=pltpu.HBM),
+            pl.BlockSpec(memory_space=pltpu.HBM),
         ],
         out_specs=pl.BlockSpec(memory_space=pltpu.VMEM),
         scratch_shapes=[
+            vmem((1, 2 * PANEL), jnp.int32),
+            vmem((1, 2), jnp.int32),
+            vmem((2, BANDS), jnp.int32),
             vmem((PANEL, PANEL), F32),
-            vmem((REACH, ROWS, PANEL), F32),
+            vmem((5, BLOCK, BLOCK), F32),
+            vmem((REACH, 5, BLOCK, BLOCK), F32),
             vmem((REACH, 1, 2 * PANEL), jnp.int32),
+            vmem((REACH, 1, 2), jnp.int32),
+            vmem((REACH, 2, BLOCK, BLOCK), F32),
+            vmem((2, BLOCK, BLOCK), F32),
+            vmem((2, BLOCK, BLOCK), F32),
+            vmem((BLOCK, PANEL), BF16),
+            vmem((BLOCK, PANEL), BF16),
             vmem((PANEL, CLASSES * PANEL), BF16),
             vmem((PANEL, CLASSES * PANEL), BF16),
             vmem((PANEL, 2 * BANDS), BF16),
@@ -362,7 +437,7 @@
             vmem((CLASSES, ROWS, 2 * BANDS), F32),
             vmem((2 * BANDS, PANEL), F32),
             vmem((2 * BANDS, 2 * BANDS), F32),
-            vmem((CHUNK_ROWS, CLASSES * PANEL), F32),
+            vmem((BLOCK, CLASSES * PANEL), F32),
             vmem((2 * BANDS, CLASSES * PANEL), F32),
             vmem((BANDS, BANDS), F32),
             vmem((2 * BANDS, 2 * BANDS), F32),
@@ -372,18 +447,19 @@
             vmem((3, 8, 128), F32),
             vmem((8, 128), F32),
             vmem((7, 8, 128), F32),
-            dma((REACH, CHUNKS)),
-            dma((REACH, CHUNKS)),
-            dma((REACH,)),
-            dma((REACH,)),
+            dma((REACH, 3)),
+            dma((REACH, 3)),
+            dma((2, REACH)),
+            dma((2, REACH)),
             dma((2,)),
-            dma,
+            dma((2,)),
+            dma((9,)),
             dma((2, 3)),
             dma((2, 3)),
             dma((2, 7)),
         ],
         compiler_params=pltpu.CompilerParams(
-            collective_id=0, has_side_effects=True, vmem_limit_bytes=48 * 1024 * 1024
+            collective_id=0, has_side_effects=True, vmem_limit_bytes=67_043_328
         ),
     )(inverse_cov, channel_keep_mask, partner_ids, band_starts)
 

time: 77 us -> 47.4 us (0.62)
  Pallas kernels: 72.9 us -> 45.8 us
  local copies, waits for them, and re-layouts: 3.9 us -> 1.38 us
    pallas_call x1, Pallas kernels: 72.9 us -> 45.8 us  [body(): pl.pallas_call(body_kernel, out_shape=jax.ShapeDtypeStruct((2, 16, 2), F3...]
    unnamed x8 -> x0, local copies, waits for them, and re-layouts: 3.24 us -> none
where the time goes in v2:
time: 47.4 us; the launch traced here: 47.2 us
  Pallas kernels  45.8 us (97%)
  local copies, waits for them, and re-layouts  1.38 us (3%)
    pallas_call x1, Pallas kernels, body(): pl.pallas_call(body_kernel, out_shape=jax.ShapeDtypeStruct((2, 16, 2), F3...  45.8 us
    pallas_call x1, local copies, waits for them, and re-layouts, body(): pl.pallas_call(body_kernel, out_shape=jax.ShapeDtypeStruct((2, 16, 2), F3...  1.38 us

profile of v2, /device:TPU:1, one launch (start us, length us, event | category | flops | bytes accessed | tf_op | source)
XLA Modules:
  0.0 47.2 jit_solution(18203007280176007066)
XLA Ops:
  0.0 45.8 %shard_map.46 = f32[2,16,2]{2,1,0:T(8,128)} custom-call(f32[1,256,1024]{2,1,0:T(8,128)} %inv_ref.1, s32[1,1024]{1,0:T(1,128)} %mask_hbm.1, s32[1,2]{1,0:T(1,128)} %partner_hbm.1, s32[2,64]{1,0:T(2,128)} %start_hbm.1), custom_call_target="tpu_custom_call" | custom-call | tf_op jit(solution)/shard_map/pallas_call | solution.py:398
  45.8 1.4 %copy.5 = f32[2,16,2]{1,2,0:T(2,128)} copy(f32[2,16,2]{2,1,0:T(8,128)} %shard_map.46) | data formatting | bytes 512 | tf_op jit(solution)/shard_map/pallas_call | solution.py:398

commit v3 on v2

--- a/solution.py
+++ b/solution.py
@@ -15,7 +15,9 @@
 REACH = 4
 SENDS = (-1, 2, -3, 4)
 BLOCK = 128
-GROUPS_OF_BLOCKS = ((0, 2), (2, 2), (4, 1))
+TILE = 256
+MESSAGES = ((0, 2, 0, 128), (2, 2, 0, 128), (4, 1, 0, 128))
+STEPS = ((0, 0, 128), (1, 0, 128))
 PANEL = 512
 ROWS = 256
 BANDS = 64
@@ -34,7 +36,9 @@
 
 
 def dot3(a, b):
-    return mm(a[0], b[0]) + (mm(a[0], b[1]) + mm(a[1], b[0]))
+    rows = a[0].shape[0]
+    both = mm(jnp.concatenate(a, axis=0), b[0])
+    return both[:rows] + (mm(a[0], b[1]) + both[rows:])
 
 
 def iota(shape, dim):
@@ -48,19 +52,17 @@
 def body_kernel(
     inv_ref, mask_hbm, partner_hbm, start_hbm, out_ref,
     mask_ref, partner_ref, start_ref, own_raw, own_pack, got, got_mask, got_partner, row_marks,
-    far_sum, got_far, rows_hi, rows_lo,
+    far_sum, got_far, turned_far, turned_corner, rows_hi, rows_lo,
     toep_hi, toep_lo, edge_hi, edge_lo, win, decay_hi, decay_lo,
     decay_t_hi, decay_t_lo, edge_t_hi, edge_t_lo, win_t, panel_hi, panel_lo, filt, filt_edge,
-    outer, outer_decay, mixed, gram, total, mirror,
-    sum_x, got_x, sum_y, got_y, sum_z, got_z,
-    send_sem, recv_sem, mask_sem, partner_sem, sib_sem, far_sem, own_sem, x_sem, y_sem, z_sem,
+    outer, outer_decay, boxes, gram, total, mirror,
+    sum_xy, got_xy, sum_z, got_z,
+    send_sem, recv_sem, mask_sem, partner_sem, sib_sem, far_sem, own_sem, xy_sem, z_sem,
 ):
     me = lax.axis_index("bl")
     part = lax.axis_index("bp")
     half = part // 2
     core = part % 2
-    pos_x = me % 4
-    pos_y = (me // 4) % 4
     pos_z = me // 16
     first = pl.multiple_of(core * ROWS, ROWS)
     col0 = pl.multiple_of(half * PANEL, PANEL)
@@ -84,11 +86,10 @@
     def lanes_of(block):
         return pl.ds(pl.multiple_of(col0 + BLOCK * block, BLOCK), BLOCK)
 
-    def x_peer(e):
-        return (me - pos_x + (pos_x + e) % 4, part)
-
-    def y_peer(e):
-        return (me - 4 * pos_y + 4 * ((pos_y + e) % 4), part)
+    plane = me % 16
+
+    def plane_peer(e):
+        return (me - plane + (plane + e) % 16, part)
 
     spot = pos_z * 4 + part
 
@@ -99,8 +100,7 @@
     peers = (
         [target(d) for d in range(REACH)]
         + [source(d) for d in range(REACH)]
-        + [x_peer(e) for e in range(1, 4)]
-        + [y_peer(e) for e in range(1, 4)]
+        + [plane_peer(e) for e in range(1, 16)]
         + [z_peer(e) for e in range(1, 8)]
     )
     barrier = pltpu.get_barrier_semaphore()
@@ -144,10 +144,11 @@
             copy.start()
             mask_copies.append(copy)
     copies = {}
-    for g, (p, count) in enumerate(GROUPS_OF_BLOCKS):
+    for g, (p, count, row0, height) in enumerate(MESSAGES):
         for d in range(REACH):
             copy = pltpu.make_async_remote_copy(
-                src_ref=own_pack.at[pl.ds(p, count)], dst_ref=got.at[d, pl.ds(p, count)],
+                src_ref=own_pack.at[pl.ds(p, count), pl.ds(row0, height)],
+                dst_ref=got.at[d, pl.ds(p, count), pl.ds(row0, height)],
                 send_sem=send_sem.at[d, g], recv_sem=recv_sem.at[d, g],
                 device_id=target(d), device_id_type=MESH,
             )
@@ -232,6 +233,7 @@
         copy.wait()
     total[...] = jnp.zeros_like(total)
     gram[...] = jnp.zeros_like(gram)
+    boxes[...] = jnp.zeros_like(boxes)
     mirror[...] = jnp.zeros_like(mirror)
     for d in range(REACH):
         if SENDS[d] < 0:
@@ -243,19 +245,19 @@
             marks = got_mask[d, :, lanes_of(near[r])].astype(F32) * weight
             row_marks[d, r] = down(marks, BLOCK)
 
-    def summed(p):
+    def summed(p, at=slice(0, BLOCK)):
         r, c = pack[p]
         out = 0.0
         for d in range(REACH):
             cols = got_mask[d, :, lanes_of(c)].astype(F32)
-            out = out + got[d, p] * row_marks[d, r] * cols
+            out = out + got[d, p, at] * row_marks[d, r, at] * cols
         return out
 
     def put(block, value):
         hi, lo = split(value)
         spot = pl.ds(pl.multiple_of(BLOCK * block, BLOCK), BLOCK)
-        rows_hi[:, spot] = hi
-        rows_lo[:, spot] = lo
+        rows_hi[: value.shape[0], spot] = hi
+        rows_lo[: value.shape[0], spot] = lo
 
     far_copy = pltpu.make_async_remote_copy(
         src_ref=far_sum, dst_ref=got_far,
@@ -266,50 +268,58 @@
     for r in range(2):
         far_sum[r] = summed(r)
     far_copy.start()
-    for k in range(2):
-        y0 = k * BLOCK
+    for step, (k, row0, height) in enumerate(STEPS):
+        y0 = k * BLOCK + row0
+        at = slice(row0, row0 + height)
         for d in range(REACH):
-            copies[d, k + 1].wait_recv()
-        if k == 0:
+            copies[d, step + 1].wait_recv()
+        if step == 0:
             far_copy.wait_recv()
-        put(far[k], far_sum[k])
-        put(missing[k], jnp.transpose(got_far[missing_slot[k]]))
+            for r in range(2):
+                turned_far[r] = jnp.transpose(got_far[missing_slot[r]])
+        put(far[k], far_sum[k, at])
+        put(missing[k], turned_far[k, at])
         if k == 0:
             put(near[0], summed(2))
             corner = summed(3)
             put(near[1], corner)
-            row_marks[0, 0] = jnp.transpose(corner)
+            turned_corner[...] = jnp.transpose(corner)
         else:
-            put(near[0], row_marks[0, 0])
-            put(near[1], summed(4))
-        rows = (rows_hi[...], rows_lo[...])
-        here = pl.ds(pl.multiple_of(first + y0, BLOCK), BLOCK)
+            put(near[0], turned_corner[at])
+            put(near[1], summed(4, at))
+        rows = (rows_hi[:height], rows_lo[:height])
+        here = pl.ds(pl.multiple_of(first + k * BLOCK, BLOCK), BLOCK)
         decay_t = (decay_t_hi[:, here], decay_t_lo[:, here])
         edges = dot3(rows, (edge_hi[...], edge_lo[...]))
         mirror[...] += dot3(decay_t, split(edges))
-        for l in range(CLASSES):
-            span = slice(l * PANEL, (l + 1) * PANEL)
-            out = dot3(rows, (toep_hi[:, span], toep_lo[:, span]))
-            mixed[:, span] = out
-            gram[:, span] += dot3(decay_t, split(out))
-        acc = jnp.zeros((BANDS, BANDS), F32)
+        rims = []
         for lb in range(CLASSES):
             rim = edges * filt_edge[lb, y0 : y0 + BLOCK, :]
-            sums = -(rim[:, :BANDS] + rim[:, BANDS:])
-            for la in range(lb + 1):
-                span = slice(la * PANEL, (la + 1) * PANEL)
-                hi, lo = split(mixed[:, span] * filt[lb, y0 : y0 + BLOCK, :])
-                sums = sums + (mm(hi, win[span, :]) + mm(lo, win[span, :]))
-            hi, lo = split(sums)
-            acc = acc + (mm(win_t[lb, :, here], hi) + mm(win_t[lb, :, here], lo))
-        total[...] += acc
-    cross = jnp.zeros((2 * BANDS, BANDS), F32)
+            rims.append(rim[:, :BANDS] + rim[:, BANDS:])
+        inside = jnp.concatenate([win_t[lb, :, here] for lb in range(CLASSES)], axis=1)
+        hi, lo = split(jnp.concatenate(rims, axis=0))
+        total[...] -= mm(inside, hi) + mm(inside, lo)
+        for la in range(CLASSES):
+            for c0 in range(0, PANEL, TILE):
+                span = slice(la * PANEL + c0, la * PANEL + c0 + TILE)
+                out = dot3(rows, (toep_hi[:, span], toep_lo[:, span]))
+                gram[:, span] += dot3(decay_t, split(out))
+                hi, lo = split(
+                    jnp.concatenate(
+                        [out * filt[lb, y0 : y0 + BLOCK, c0 : c0 + TILE] for lb in range(la, CLASSES)],
+                        axis=0,
+                    )
+                )
+                above = inside[:, la * BLOCK :]
+                boxes[:, span] += mm(above, hi) + mm(above, lo)
+    fisher = total[...]
     for la in range(CLASSES):
         span = slice(la * PANEL, (la + 1) * PANEL)
-        hi, lo = split(gram[:, span] * outer[...])
-        cross = cross + (mm(hi, win[span, :]) + mm(lo, win[span, :]))
+        left = gram[:BANDS, span] * outer[:BANDS, :]
+        right = gram[BANDS:, span] * outer[BANDS:, :]
+        hi, lo = split(boxes[:, span] - (left + right))
+        fisher = fisher + (mm(hi, win[span, :]) + mm(lo, win[span, :]))
     four = mirror[...] * outer_decay[...]
-    fisher = total[...] - cross[:BANDS] - cross[BANDS:]
     fisher = fisher + (four[:BANDS, :BANDS] + four[:BANDS, BANDS:])
     fisher = fisher + (four[BANDS:, :BANDS] + four[BANDS:, BANDS:])
     row_class = iota((BANDS, BANDS), 0) % CLASSES
@@ -319,9 +329,9 @@
     turned_over = jnp.transpose(jnp.concatenate([wide, jnp.zeros_like(wide)], axis=0))
     fisher = kept + jnp.where(col_class > row_class, turned_over[:BANDS, :BANDS], 0.0)
 
-    row = iota((BANDS // 2, BANDS), 0)
-    owner = (row % 2) * 16 + ((row // 2) % 4) * 4 + row // 8
-    col = iota((BANDS // 2, BANDS), 1)
+    row = iota((128, BANDS), 0)
+    owner = (row % 8) * 16 + row // 8
+    col = iota((128, BANDS), 1)
     parts3 = []
     rest = fisher
     for _ in range(3):
@@ -333,35 +343,21 @@
         pick = jnp.where(col == 2 * owner + side, 1.0, 0.0).astype(BF16)
         turned.append(mm(pick, parts3[0]) + mm(pick, parts3[1]) + mm(pick, parts3[2]))
     placed = jnp.concatenate(turned, axis=1)
-    for x in range(4):
-        sum_x[x] = placed[8 * x : 8 * x + 8]
-
-    x_copies = []
-    for e in range(1, 4):
+    sum_xy[...] = placed.reshape(16, 8, 128)
+
+    xy_copies = []
+    for e in range(1, 16):
         copy = pltpu.make_async_remote_copy(
-            src_ref=sum_x.at[(pos_x + e) % 4], dst_ref=got_x.at[e - 1],
-            send_sem=x_sem.at[0, e - 1], recv_sem=x_sem.at[1, e - 1],
-            device_id=x_peer(e), device_id_type=MESH,
+            src_ref=sum_xy.at[(plane + e) % 16], dst_ref=got_xy.at[e - 1],
+            send_sem=xy_sem.at[0, e - 1], recv_sem=xy_sem.at[1, e - 1],
+            device_id=plane_peer(e), device_id_type=MESH,
         )
         copy.start()
-        x_copies.append(copy)
-    tile = sum_x[pos_x]
-    for e in range(3):
-        x_copies[e].wait_recv()
-        tile = tile + got_x[e]
-    sum_y[...] = tile
-    y_copies = []
-    for e in range(1, 4):
-        copy = pltpu.make_async_remote_copy(
-            src_ref=sum_y, dst_ref=got_y.at[e - 1],
-            send_sem=y_sem.at[0, e - 1], recv_sem=y_sem.at[1, e - 1],
-            device_id=y_peer(e), device_id_type=MESH,
-        )
-        copy.start()
-        y_copies.append(copy)
-    for e in range(3):
-        y_copies[e].wait_recv()
-        tile = tile + got_y[e]
+        xy_copies.append(copy)
+    tile = sum_xy[plane]
+    for e in range(15):
+        xy_copies[e].wait_recv()
+        tile = tile + got_xy[e]
     sum_z[...] = tile
     z_copies = []
     for e in range(1, 8):
@@ -378,26 +374,23 @@
         from_half = ((spot + 7 - e) % 8 % 4) // 2
         for h in range(2):
             halves[h] = halves[h] + jnp.where(from_half == h, got_z[e], 0.0)
-    my_row = pos_y * 2 + pos_z
-    lanes = iota((16, 128), 1)
+    lanes = iota((2, 16, 128), 2)
+    band = 16 * part + iota((2, 16, 128), 1) + BANDS * iota((2, 16, 128), 0)
     for h in range(2):
-        line = jnp.sum(jnp.where(iota((8, 128), 0) == my_row, halves[h], 0.0), axis=0, keepdims=True)
-        line = jnp.broadcast_to(line, (16, 128))
-        band = 16 * part + iota((16, 128), 0)
-        for side in range(2):
-            one = jnp.where(lanes == band + side * BANDS, line, 0.0)
-            out_ref[h, :, side : side + 1] = jnp.sum(one, axis=1, keepdims=True)
-
-    for copy in list(copies.values()) + [far_copy] + x_copies + y_copies + z_copies:
+        line = jnp.where(pos_z == 0, halves[h][0:1], halves[h][1:2])
+        line = jnp.broadcast_to(line[None], (2, 16, 128))
+        out_ref[h] = jnp.sum(jnp.where(lanes == band, line, 0.0), axis=2)
+
+    for copy in list(copies.values()) + [far_copy] + xy_copies + z_copies:
         copy.wait_send()
 
 
 def body(inverse_cov, channel_keep_mask, partner_ids, band_starts):
     vmem = pltpu.VMEM
     dma = pltpu.SemaphoreType.DMA
-    return pl.pallas_call(
+    out = pl.pallas_call(
         body_kernel,
-        out_shape=jax.ShapeDtypeStruct((2, 16, 2), F32),
+        out_shape=jax.ShapeDtypeStruct((2, 2, 16), F32),
         in_specs=[
             pl.BlockSpec(memory_space=pltpu.HBM),
             pl.BlockSpec(memory_space=pltpu.HBM),
@@ -417,6 +410,8 @@
             vmem((REACH, 2, BLOCK, BLOCK), F32),
             vmem((2, BLOCK, BLOCK), F32),
             vmem((2, BLOCK, BLOCK), F32),
+            vmem((2, BLOCK, BLOCK), F32),
+            vmem((BLOCK, BLOCK), F32),
             vmem((BLOCK, PANEL), BF16),
             vmem((BLOCK, PANEL), BF16),
             vmem((PANEL, CLASSES * PANEL), BF16),
@@ -437,31 +432,29 @@
             vmem((CLASSES, ROWS, 2 * BANDS), F32),
             vmem((2 * BANDS, PANEL), F32),
             vmem((2 * BANDS, 2 * BANDS), F32),
-            vmem((BLOCK, CLASSES * PANEL), F32),
+            vmem((BANDS, CLASSES * PANEL), F32),
             vmem((2 * BANDS, CLASSES * PANEL), F32),
             vmem((BANDS, BANDS), F32),
             vmem((2 * BANDS, 2 * BANDS), F32),
-            vmem((4, 8, 128), F32),
-            vmem((3, 8, 128), F32),
-            vmem((8, 128), F32),
-            vmem((3, 8, 128), F32),
+            vmem((16, 8, 128), F32),
+            vmem((15, 8, 128), F32),
             vmem((8, 128), F32),
             vmem((7, 8, 128), F32),
-            dma((REACH, 3)),
-            dma((REACH, 3)),
+            dma((REACH, len(MESSAGES))),
+            dma((REACH, len(MESSAGES))),
             dma((2, REACH)),
             dma((2, REACH)),
             dma((2,)),
             dma((2,)),
             dma((9,)),
-            dma((2, 3)),
-            dma((2, 3)),
+            dma((2, 15)),
             dma((2, 7)),
         ],
         compiler_params=pltpu.CompilerParams(
             collective_id=0, has_side_effects=True, vmem_limit_bytes=67_043_328
         ),
     )(inverse_cov, channel_keep_mask, partner_ids, band_starts)
+    return jnp.transpose(out, (0, 2, 1))
 
 
 def solution(mesh):

time: 47.4 us -> 44.4 us (0.937)
  Pallas kernels: 45.8 us -> 43 us
    pallas_call x1, Pallas kernels: 45.8 us -> 43 us  [body(): pl.pallas_call(body_kernel, out_shape=jax.ShapeDtypeStruct((2, 2, 16), F3...]
    pallas_call x1 -> x0, local copies, waits for them, and re-layouts: 1.38 us -> none  [body(): pl.pallas_call(body_kernel, out_shape=jax.ShapeDtypeStruct((2, 16, 2), F3...]
    unnamed x0 -> x1, local copies, waits for them, and re-layouts: none -> 1.26 us
where the time goes in v3:
time: 44.4 us; the launch traced here: 44.3 us
  Pallas kernels  43 us (97%)
  local copies, waits for them, and re-layouts  1.26 us (3%)
    pallas_call x1, Pallas kernels, body(): pl.pallas_call(body_kernel, out_shape=jax.ShapeDtypeStruct((2, 2, 16), F3...  43 us
    unnamed x1, local copies, waits for them, and re-layouts  1.26 us

profile of v3, /device:TPU:1, one launch (start us, length us, event | category | flops | bytes accessed | tf_op | source)
XLA Modules:
  0.0 44.3 jit_solution(3752065314151204485)
XLA Ops:
  0.0 43.0 %shard_map.46 = f32[2,2,16]{2,1,0:T(2,128)} custom-call(f32[1,256,1024]{2,1,0:T(8,128)} %inv_ref.1, s32[1,1024]{1,0:T(1,128)} %mask_hbm.1, s32[1,2]{1,0:T(1,128)} %partner_hbm.1, s32[2,64]{1,0:T(2,128)} %start_hbm.1), custom_call_target="tpu_custom_call" | custom-call | tf_op jit(solution)/shard_map/pallas_call | solution.py:391
  43.0 1.3 %copy.6 = f32[2,16,2]{1,2,0:T(2,128)} copy(f32[2,16,2]{1,2,0:T(2,128)} %bitcast.1) | data formatting | bytes 512

commit v4 on v3

--- a/solution.py
+++ b/solution.py
@@ -16,8 +16,7 @@
 SENDS = (-1, 2, -3, 4)
 BLOCK = 128
 TILE = 256
-MESSAGES = ((0, 2, 0, 128), (2, 2, 0, 128), (4, 1, 0, 128))
-STEPS = ((0, 0, 128), (1, 0, 128))
+MESSAGES = ((0, 2), (2, 2), (4, 1))
 PANEL = 512
 ROWS = 256
 BANDS = 64
@@ -52,7 +51,7 @@
 def body_kernel(
     inv_ref, mask_hbm, partner_hbm, start_hbm, out_ref,
     mask_ref, partner_ref, start_ref, own_raw, own_pack, got, got_mask, got_partner, row_marks,
-    far_sum, got_far, turned_far, turned_corner, rows_hi, rows_lo,
+    far_sum, got_far, far_edges, far_out, turned_corner, rows_hi, rows_lo,
     toep_hi, toep_lo, edge_hi, edge_lo, win, decay_hi, decay_lo,
     decay_t_hi, decay_t_lo, edge_t_hi, edge_t_lo, win_t, panel_hi, panel_lo, filt, filt_edge,
     outer, outer_decay, boxes, gram, total, mirror,
@@ -103,10 +102,6 @@
         + [plane_peer(e) for e in range(1, 16)]
         + [z_peer(e) for e in range(1, 8)]
     )
-    barrier = pltpu.get_barrier_semaphore()
-    for peer in peers:
-        pl.semaphore_signal(barrier, inc=1, device_id=peer, device_id_type=MESH)
-
     locals_ = [
         pltpu.make_async_copy(
             inv_ref.at[0, BLOCK * r : BLOCK * (r + 1), lanes_of(c)], own_pack.at[p], own_sem.at[p]
@@ -122,15 +117,14 @@
     locals_.append(pltpu.make_async_copy(start_hbm, start_ref, own_sem.at[8]))
     for copy in locals_:
         copy.start()
-    for copy in locals_:
-        copy.wait()
+    barrier = pltpu.get_barrier_semaphore()
+    for peer in peers:
+        pl.semaphore_signal(barrier, inc=1, device_id=peer, device_id_type=MESH)
+
+    for n in (0, 1, 6, 7):
+        locals_[n].wait()
     pl.semaphore_wait(barrier, len(peers))
 
-    sib_copy = pltpu.make_async_remote_copy(
-        src_ref=own_rows, dst_ref=own_rows,
-        send_sem=sib_sem.at[0], recv_sem=sib_sem.at[1], device_id=sibling, device_id_type=MESH,
-    )
-    sib_copy.start()
     mask_copies = []
     for d in range(REACH):
         pairs = [(mask_ref, got_mask, mask_sem)]
@@ -144,17 +138,27 @@
             copy.start()
             mask_copies.append(copy)
     copies = {}
-    for g, (p, count, row0, height) in enumerate(MESSAGES):
+    for g, (p, count) in enumerate(MESSAGES):
+        if g:
+            for n in range(p, p + count):
+                locals_[n].wait()
         for d in range(REACH):
             copy = pltpu.make_async_remote_copy(
-                src_ref=own_pack.at[pl.ds(p, count), pl.ds(row0, height)],
-                dst_ref=got.at[d, pl.ds(p, count), pl.ds(row0, height)],
+                src_ref=own_pack.at[pl.ds(p, count)],
+                dst_ref=got.at[d, pl.ds(p, count)],
                 send_sem=send_sem.at[d, g], recv_sem=recv_sem.at[d, g],
                 device_id=target(d), device_id_type=MESH,
             )
             copy.start()
             copies[d, g] = copy
-
+    locals_[5].wait()
+    sib_copy = pltpu.make_async_remote_copy(
+        src_ref=own_rows, dst_ref=own_rows,
+        send_sem=sib_sem.at[0], recv_sem=sib_sem.at[1], device_id=sibling, device_id_type=MESH,
+    )
+    sib_copy.start()
+
+    locals_[8].wait()
     starts = start_ref[pl.ds(half, 1), :]
     starts2 = jnp.concatenate([starts, starts], axis=1)
     lane = iota((1, 2 * BANDS), 1)
@@ -168,7 +172,15 @@
         inside = (from_start >= 0) & (to_end >= 0)
         gap = jnp.where(is_left, -from_start, -to_end)
         edge = jnp.where(gap > 0, jnp.exp(-jnp.abs(gap).astype(F32) * rate), 0.0)
-        edge_hi[r0 : r0 + 128, :], edge_lo[r0 : r0 + 128, :] = split(edge)
+        edge_hi[r0 : r0 + 128, : 2 * BANDS], edge_lo[r0 : r0 + 128, : 2 * BANDS] = split(edge)
+        side_lane = iota((128, 2 * BANDS), 1)
+        low_half = (side_lane + core) % 2 == 1
+        reach = jnp.where(low_half, TILE - 1 - pos, pos - TILE)
+        side_rate = 1.0 / (1 + (side_lane // 2) % CLASSES).astype(F32)
+        spill = jnp.where(
+            (reach >= 0) & (side_lane < 2 * CLASSES), jnp.exp(-jnp.abs(reach).astype(F32) * side_rate), 0.0
+        )
+        edge_hi[r0 : r0 + 128, 2 * BANDS :], edge_lo[r0 : r0 + 128, 2 * BANDS :] = split(spill)
         decay = jnp.where(inside, jnp.exp(-jnp.abs(gap).astype(F32) * rate), 0.0)
         decay_hi[r0 : r0 + 128, :], decay_lo[r0 : r0 + 128, :] = split(decay)
         for l in range(CLASSES):
@@ -232,8 +244,8 @@
     for copy in mask_copies:
         copy.wait()
     total[...] = jnp.zeros_like(total)
+    boxes[...] = jnp.zeros_like(boxes)
     gram[...] = jnp.zeros_like(gram)
-    boxes[...] = jnp.zeros_like(boxes)
     mirror[...] = jnp.zeros_like(mirror)
     for d in range(REACH):
         if SENDS[d] < 0:
@@ -245,19 +257,20 @@
             marks = got_mask[d, :, lanes_of(near[r])].astype(F32) * weight
             row_marks[d, r] = down(marks, BLOCK)
 
-    def summed(p, at=slice(0, BLOCK)):
+    def summed(p):
         r, c = pack[p]
         out = 0.0
         for d in range(REACH):
             cols = got_mask[d, :, lanes_of(c)].astype(F32)
-            out = out + got[d, p, at] * row_marks[d, r, at] * cols
+            out = out + got[d, p] * row_marks[d, r] * cols
         return out
 
-    def put(block, value):
-        hi, lo = split(value)
-        spot = pl.ds(pl.multiple_of(BLOCK * block, BLOCK), BLOCK)
-        rows_hi[: value.shape[0], spot] = hi
-        rows_lo[: value.shape[0], spot] = lo
+    def filtered(rows, l):
+        square = slice(l * PANEL, l * PANEL + TILE)
+        return dot3(rows, (toep_hi[:TILE, square], toep_lo[:TILE, square]))
+
+    near_half = pl.ds(first, TILE)
+    far_half = pl.ds(pl.multiple_of(TILE - first, TILE), TILE)
 
     far_copy = pltpu.make_async_remote_copy(
         src_ref=far_sum, dst_ref=got_far,
@@ -268,58 +281,89 @@
     for r in range(2):
         far_sum[r] = summed(r)
     far_copy.start()
-    for step, (k, row0, height) in enumerate(STEPS):
-        y0 = k * BLOCK + row0
-        at = slice(row0, row0 + height)
+    far_copy.wait_recv()
+    far_block = 2 - 2 * core
+    for r in range(2):
+        for block, value in (
+            (far[r], far_sum[r]), (missing[r], jnp.transpose(got_far[missing_slot[r]]))
+        ):
+            lanes_at = pl.ds(pl.multiple_of(BLOCK * (block - far_block), BLOCK), BLOCK)
+            hi, lo = split(value)
+            rows_hi[r * BLOCK : (r + 1) * BLOCK, lanes_at] = hi
+            rows_lo[r * BLOCK : (r + 1) * BLOCK, lanes_at] = lo
+    rows = (rows_hi[...], rows_lo[...])
+    far_edges[...] = dot3(rows, (edge_hi[far_half, :], edge_lo[far_half, :]))
+    far_gram = dot3((decay_t_hi[:, near_half], decay_t_lo[:, near_half]), rows)
+    gram_hi, gram_lo = split(far_gram)
+    stack = tuple(jnp.concatenate(pair, axis=0) for pair in ((rows[0], gram_hi), (rows[1], gram_lo)))
+    for l in range(CLASSES):
+        far_out[:, l * TILE : (l + 1) * TILE] = filtered(stack, l)
+
+    in_low = core == 0
+    tile_lane = iota((1, TILE), 1).astype(F32)
+    rises = []
+    for l in range(CLASSES):
+        to_low = jnp.exp((tile_lane - TILE) * (1.0 / (1 + l)))
+        to_high = jnp.exp((tile_lane + 1.0) * (-1.0 / (1 + l)))
+        rises.append((jnp.where(in_low, to_low, to_high), jnp.where(in_low, to_high, to_low)))
+    for k in range(2):
+        y0 = k * BLOCK
         for d in range(REACH):
-            copies[d, step + 1].wait_recv()
-        if step == 0:
-            far_copy.wait_recv()
-            for r in range(2):
-                turned_far[r] = jnp.transpose(got_far[missing_slot[r]])
-        put(far[k], far_sum[k, at])
-        put(missing[k], turned_far[k, at])
+            copies[d, k + 1].wait_recv()
         if k == 0:
-            put(near[0], summed(2))
             corner = summed(3)
-            put(near[1], corner)
+            blocks = (summed(2), corner)
             turned_corner[...] = jnp.transpose(corner)
         else:
-            put(near[0], turned_corner[at])
-            put(near[1], summed(4, at))
-        rows = (rows_hi[:height], rows_lo[:height])
-        here = pl.ds(pl.multiple_of(first + k * BLOCK, BLOCK), BLOCK)
+            blocks = (turned_corner[...], summed(4))
+        rows = split(jnp.concatenate(blocks, axis=1))
+        here = pl.ds(pl.multiple_of(first + y0, BLOCK), BLOCK)
         decay_t = (decay_t_hi[:, here], decay_t_lo[:, here])
-        edges = dot3(rows, (edge_hi[...], edge_lo[...]))
+        edges = far_edges[y0 : y0 + BLOCK, :] + dot3(rows, (edge_hi[near_half, :], edge_lo[near_half, :]))
         mirror[...] += dot3(decay_t, split(edges))
+        gram[...] += dot3(decay_t, rows)
+        stack = rows
+        if k == 1:
+            near_gram = split(gram[...])
+            stack = tuple(jnp.concatenate((a, b), axis=0) for a, b in zip(rows, near_gram))
         rims = []
         for lb in range(CLASSES):
-            rim = edges * filt_edge[lb, y0 : y0 + BLOCK, :]
+            rim = edges[:, : 2 * BANDS] * filt_edge[lb, y0 : y0 + BLOCK, :]
             rims.append(rim[:, :BANDS] + rim[:, BANDS:])
         inside = jnp.concatenate([win_t[lb, :, here] for lb in range(CLASSES)], axis=1)
         hi, lo = split(jnp.concatenate(rims, axis=0))
         total[...] -= mm(inside, hi) + mm(inside, lo)
         for la in range(CLASSES):
-            for c0 in range(0, PANEL, TILE):
-                span = slice(la * PANEL + c0, la * PANEL + c0 + TILE)
-                out = dot3(rows, (toep_hi[:, span], toep_lo[:, span]))
-                gram[:, span] += dot3(decay_t, split(out))
+            near_out = filtered(stack, la)
+            above = inside[:, la * BLOCK :]
+            tile = slice(la * TILE, (la + 1) * TILE)
+            for j, half_cols in enumerate((near_half, far_half)):
+                lane_col = 2 * BANDS + 2 * la + j
+
+                def square(own, far_rows, source):
+                    plain = near_out[own : own + BLOCK] if j == 0 else far_out[far_rows, tile]
+                    return plain + source[:, lane_col : lane_col + 1] * rises[la][j]
+
+                out = square(0, slice(y0, y0 + BLOCK), edges)
                 hi, lo = split(
                     jnp.concatenate(
-                        [out * filt[lb, y0 : y0 + BLOCK, c0 : c0 + TILE] for lb in range(la, CLASSES)],
+                        [out * filt[lb, y0 : y0 + BLOCK, half_cols] for lb in range(la, CLASSES)],
                         axis=0,
                     )
                 )
-                above = inside[:, la * BLOCK :]
-                boxes[:, span] += mm(above, hi) + mm(above, lo)
+                box = mm(above, hi) + mm(above, lo)
+                if k == 1:
+                    rim = square(BLOCK, slice(2 * BLOCK, 3 * BLOCK), mirror[...]) * outer[:, half_cols]
+                    box = box - (rim[:BANDS] + rim[BANDS:])
+                span = slice(la * PANEL + j * TILE, la * PANEL + (j + 1) * TILE)
+                boxes[:, span] += box
     fisher = total[...]
     for la in range(CLASSES):
-        span = slice(la * PANEL, (la + 1) * PANEL)
-        left = gram[:BANDS, span] * outer[:BANDS, :]
-        right = gram[BANDS:, span] * outer[BANDS:, :]
-        hi, lo = split(boxes[:, span] - (left + right))
-        fisher = fisher + (mm(hi, win[span, :]) + mm(lo, win[span, :]))
-    four = mirror[...] * outer_decay[...]
+        for j, half_first in enumerate((first, TILE - first)):
+            hi, lo = split(boxes[:, la * PANEL + j * TILE : la * PANEL + (j + 1) * TILE])
+            channels = win[pl.ds(pl.multiple_of(la * PANEL + half_first, TILE), TILE), :]
+            fisher = fisher + (mm(hi, channels) + mm(lo, channels))
+    four = mirror[:, : 2 * BANDS] * outer_decay[...]
     fisher = fisher + (four[:BANDS, :BANDS] + four[:BANDS, BANDS:])
     fisher = fisher + (four[BANDS:, :BANDS] + four[BANDS:, BANDS:])
     row_class = iota((BANDS, BANDS), 0) % CLASSES
@@ -410,14 +454,15 @@
             vmem((REACH, 2, BLOCK, BLOCK), F32),
             vmem((2, BLOCK, BLOCK), F32),
             vmem((2, BLOCK, BLOCK), F32),
-            vmem((2, BLOCK, BLOCK), F32),
+            vmem((ROWS, 4 * BANDS), F32),
+            vmem((ROWS + 2 * BANDS, CLASSES * TILE), F32),
             vmem((BLOCK, BLOCK), F32),
-            vmem((BLOCK, PANEL), BF16),
-            vmem((BLOCK, PANEL), BF16),
+            vmem((ROWS, TILE), BF16),
+            vmem((ROWS, TILE), BF16),
             vmem((PANEL, CLASSES * PANEL), BF16),
             vmem((PANEL, CLASSES * PANEL), BF16),
-            vmem((PANEL, 2 * BANDS), BF16),
-            vmem((PANEL, 2 * BANDS), BF16),
+            vmem((PANEL, 4 * BANDS), BF16),
+            vmem((PANEL, 4 * BANDS), BF16),
             vmem((CLASSES * PANEL, BANDS), BF16),
             vmem((PANEL, 2 * BANDS), BF16),
             vmem((PANEL, 2 * BANDS), BF16),
@@ -433,9 +478,9 @@
             vmem((2 * BANDS, PANEL), F32),
             vmem((2 * BANDS, 2 * BANDS), F32),
             vmem((BANDS, CLASSES * PANEL), F32),
-            vmem((2 * BANDS, CLASSES * PANEL), F32),
+            vmem((2 * BANDS, TILE), F32),
             vmem((BANDS, BANDS), F32),
-            vmem((2 * BANDS, 2 * BANDS), F32),
+            vmem((2 * BANDS, 4 * BANDS), F32),
             vmem((16, 8, 128), F32),
             vmem((15, 8, 128), F32),
             vmem((8, 128), F32),

time: 44.4 us -> 41.8 us (0.941)
  Pallas kernels: 43 us -> 40.4 us
    pallas_call x1, Pallas kernels: 43 us -> 40.4 us  [body(): pl.pallas_call(body_kernel, out_shape=jax.ShapeDtypeStruct((2, 2, 16), F3...]
where the time goes in v4:
time: 41.8 us; the launch traced here: 41.6 us
  Pallas kernels  40.4 us (97%)
  local copies, waits for them, and re-layouts  1.26 us (3%)
    pallas_call x1, Pallas kernels, body(): pl.pallas_call(body_kernel, out_shape=jax.ShapeDtypeStruct((2, 2, 16), F3...  40.4 us
    unnamed x1, local copies, waits for them, and re-layouts  1.26 us

profile of v4, /device:TPU:1, one launch (start us, length us, event | category | flops | bytes accessed | tf_op | source)
XLA Modules:
  0.0 41.6 jit_solution(17724216244208396630)
XLA Ops:
  0.0 40.4 %shard_map.46 = f32[2,2,16]{2,1,0:T(2,128)} custom-call(f32[1,256,1024]{2,1,0:T(8,128)} %inv_ref.1, s32[1,1024]{1,0:T(1,128)} %mask_hbm.1, s32[1,2]{1,0:T(1,128)} %partner_hbm.1, s32[2,64]{1,0:T(2,128)} %start_hbm.1), custom_call_target="tpu_custom_call" | custom-call | tf_op jit(solution)/shard_map/pallas_call | solution.py:435
  40.4 1.3 %copy.6 = f32[2,16,2]{1,2,0:T(2,128)} copy(f32[2,16,2]{1,2,0:T(2,128)} %bitcast.1) | data formatting | bytes 512

commit v5 on v4

--- a/solution.py
+++ b/solution.py
@@ -102,6 +102,9 @@
         + [plane_peer(e) for e in range(1, 16)]
         + [z_peer(e) for e in range(1, 8)]
     )
+    barrier = pltpu.get_barrier_semaphore()
+    for peer in peers[: 2 * REACH]:
+        pl.semaphore_signal(barrier, inc=1, device_id=peer, device_id_type=MESH)
     locals_ = [
         pltpu.make_async_copy(
             inv_ref.at[0, BLOCK * r : BLOCK * (r + 1), lanes_of(c)], own_pack.at[p], own_sem.at[p]
@@ -117,10 +120,8 @@
     locals_.append(pltpu.make_async_copy(start_hbm, start_ref, own_sem.at[8]))
     for copy in locals_:
         copy.start()
-    barrier = pltpu.get_barrier_semaphore()
-    for peer in peers:
+    for peer in peers[2 * REACH :]:
         pl.semaphore_signal(barrier, inc=1, device_id=peer, device_id_type=MESH)
-
     for n in (0, 1, 6, 7):
         locals_[n].wait()
     pl.semaphore_wait(barrier, len(peers))
@@ -373,9 +374,9 @@
     turned_over = jnp.transpose(jnp.concatenate([wide, jnp.zeros_like(wide)], axis=0))
     fisher = kept + jnp.where(col_class > row_class, turned_over[:BANDS, :BANDS], 0.0)
 
-    row = iota((128, BANDS), 0)
-    owner = (row % 8) * 16 + row // 8
-    col = iota((128, BANDS), 1)
+    row = iota((BANDS // 2, BANDS), 0)
+    owner = (row % 2) * 16 + row // 2
+    col = iota((BANDS // 2, BANDS), 1)
     parts3 = []
     rest = fisher
     for _ in range(3):
@@ -387,7 +388,8 @@
         pick = jnp.where(col == 2 * owner + side, 1.0, 0.0).astype(BF16)
         turned.append(mm(pick, parts3[0]) + mm(pick, parts3[1]) + mm(pick, parts3[2]))
     placed = jnp.concatenate(turned, axis=1)
-    sum_xy[...] = placed.reshape(16, 8, 128)
+    for j in range(16):
+        sum_xy[j] = placed[2 * j : 2 * j + 2]
 
     xy_copies = []
     for e in range(1, 16):
@@ -402,39 +404,42 @@
     for e in range(15):
         xy_copies[e].wait_recv()
         tile = tile + got_xy[e]
-    sum_z[...] = tile
+    sum_z[0] = tile[0:1]
+    sum_z[1] = tile[1:2]
     z_copies = []
     for e in range(1, 8):
         copy = pltpu.make_async_remote_copy(
-            src_ref=sum_z, dst_ref=got_z.at[e - 1],
+            src_ref=sum_z.at[(spot + e) % 8 // 4], dst_ref=got_z.at[e - 1],
             send_sem=z_sem.at[0, e - 1], recv_sem=z_sem.at[1, e - 1],
             device_id=z_peer(e), device_id_type=MESH,
         )
         copy.start()
         z_copies.append(copy)
-    halves = [jnp.where(half == h, tile, 0.0) for h in range(2)]
+    mine = jnp.where(pos_z == 0, tile[0:1], tile[1:2])
+    halves = [jnp.where(half == h, mine, 0.0) for h in range(2)]
     for e in range(7):
         z_copies[e].wait_recv()
         from_half = ((spot + 7 - e) % 8 % 4) // 2
         for h in range(2):
             halves[h] = halves[h] + jnp.where(from_half == h, got_z[e], 0.0)
-    lanes = iota((2, 16, 128), 2)
-    band = 16 * part + iota((2, 16, 128), 1) + BANDS * iota((2, 16, 128), 0)
+    lanes = iota((16, 128), 1)
+    band = 16 * part + iota((16, 128), 0)
     for h in range(2):
-        line = jnp.where(pos_z == 0, halves[h][0:1], halves[h][1:2])
-        line = jnp.broadcast_to(line[None], (2, 16, 128))
-        out_ref[h] = jnp.sum(jnp.where(lanes == band, line, 0.0), axis=2)
+        line = jnp.broadcast_to(halves[h], (16, 128))
+        for side in range(2):
+            one = jnp.where(lanes == band + side * BANDS, line, 0.0)
+            out_ref[h, :, side : side + 1] = jnp.sum(one, axis=1, keepdims=True)
 
     for copy in list(copies.values()) + [far_copy] + xy_copies + z_copies:
         copy.wait_send()
 
 
-def body(inverse_cov, channel_keep_mask, partner_ids, band_starts):
+def body(*args):
     vmem = pltpu.VMEM
     dma = pltpu.SemaphoreType.DMA
-    out = pl.pallas_call(
+    return pl.pallas_call(
         body_kernel,
-        out_shape=jax.ShapeDtypeStruct((2, 2, 16), F32),
+        out_shape=jax.ShapeDtypeStruct((2, 16, 2), F32),
         in_specs=[
             pl.BlockSpec(memory_space=pltpu.HBM),
             pl.BlockSpec(memory_space=pltpu.HBM),
@@ -481,10 +486,10 @@
             vmem((2 * BANDS, TILE), F32),
             vmem((BANDS, BANDS), F32),
             vmem((2 * BANDS, 4 * BANDS), F32),
-            vmem((16, 8, 128), F32),
-            vmem((15, 8, 128), F32),
-            vmem((8, 128), F32),
-            vmem((7, 8, 128), F32),
+            vmem((16, 2, 128), F32),
+            vmem((15, 2, 128), F32),
+            vmem((2, 1, 128), F32),
+            vmem((7, 1, 128), F32),
             dma((REACH, len(MESSAGES))),
             dma((REACH, len(MESSAGES))),
             dma((2, REACH)),
@@ -496,10 +501,9 @@
             dma((2, 7)),
         ],
         compiler_params=pltpu.CompilerParams(
-            collective_id=0, has_side_effects=True, vmem_limit_bytes=67_043_328
+            collective_id=0, has_side_effects=True, vmem_limit_bytes=48 * 1024 * 1024
         ),
-    )(inverse_cov, channel_keep_mask, partner_ids, band_starts)
-    return jnp.transpose(out, (0, 2, 1))
+    )(*(pltpu.with_memory_space_constraint(x, pltpu.HBM) for x in args))
 
 
 def solution(mesh):

time: 41.8 us -> 40.1 us (0.959)
  Pallas kernels: 40.4 us -> 39.3 us
  local copies, waits for them, and re-layouts: 1.26 us -> 0.66 us
    unnamed x1 -> x0, local copies, waits for them, and re-layouts: 1.26 us -> none
    pallas_call x1, Pallas kernels: 40.4 us -> 39.3 us  [body(): pl.pallas_call(body_kernel, out_shape=jax.ShapeDtypeStruct((2, 16, 2), F3...]
    pallas_call x0 -> x1, local copies, waits for them, and re-layouts: none -> 0.66 us  [body(): pl.pallas_call(body_kernel, out_shape=jax.ShapeDtypeStruct((2, 16, 2), F3...]
where the time goes in v5:
time: 40.1 us; the launch traced here: 40 us
  Pallas kernels  39.3 us (98%)
  local copies, waits for them, and re-layouts  0.66 us (2%)
    pallas_call x1, Pallas kernels, body(): pl.pallas_call(body_kernel, out_shape=jax.ShapeDtypeStruct((2, 16, 2), F3...  39.3 us

profile of v5, /device:TPU:1, one launch (start us, length us, event | category | flops | bytes accessed | tf_op | source)
XLA Modules:
  0.0 40.0 jit_solution(16416172858651707254)
XLA Ops:
  0.0 39.3 %shard_map.46 = f32[2,16,2]{2,1,0:T(8,128)S(1)} custom-call(f32[1,256,1024]{2,1,0:T(8,128)} %inv_ref.1, s32[1,1024]{1,0:T(1,128)} %mask_hbm.1, s32[1,2]{1,0:T(1,128)} %partner_hbm.1, s32[2,64]{1,0:T(2,128)} %start_hbm.1), custom_call_target="tpu_custom_call" | custom-call | tf_op jit(solution)/shard_map/pallas_call | solution.py:440
  39.3 0.7 %copy.5 = f32[2,16,2]{1,2,0:T(2,128)} copy(f32[2,16,2]{2,1,0:T(8,128)S(1)} %shard_map.46) | data formatting | bytes 512 | tf_op jit(solution)/shard_map/pallas_call | solution.py:440

commit v6 on v5

--- a/solution.py
+++ b/solution.py
@@ -16,7 +16,7 @@
 SENDS = (-1, 2, -3, 4)
 BLOCK = 128
 TILE = 256
-MESSAGES = ((0, 2), (2, 2), (4, 1))
+HALF = BLOCK // 2
 PANEL = 512
 ROWS = 256
 BANDS = 64
@@ -50,8 +50,8 @@
 
 def body_kernel(
     inv_ref, mask_hbm, partner_hbm, start_hbm, out_ref,
-    mask_ref, partner_ref, start_ref, own_raw, own_pack, got, got_mask, got_partner, row_marks,
-    far_sum, got_far, far_edges, far_out, turned_corner, rows_hi, rows_lo,
+    mask_ref, partner_ref, start_ref, own_raw, own_pack, own_low, got, got_low, got_mask, got_partner, row_marks,
+    far_sum, got_far, far_edges, far_out, filt_rise, outer_rise, turned_corner, rows_hi, rows_lo,
     toep_hi, toep_lo, edge_hi, edge_lo, win, decay_hi, decay_lo,
     decay_t_hi, decay_t_lo, edge_t_hi, edge_t_lo, win_t, panel_hi, panel_lo, filt, filt_edge,
     outer, outer_decay, boxes, gram, total, mirror,
@@ -122,8 +122,13 @@
         copy.start()
     for peer in peers[2 * REACH :]:
         pl.semaphore_signal(barrier, inc=1, device_id=peer, device_id_type=MESH)
-    for n in (0, 1, 6, 7):
+    for n in (0, 1, 2, 4, 6, 7):
         locals_[n].wait()
+    lower = iota((HALF // 2, BLOCK), 1) < HALF
+    for n, p in enumerate((2, 4)):
+        upper_rows = own_pack[p, HALF : HALF + HALF // 2, :]
+        lower_rows = own_pack[p, HALF + HALF // 2 :, :]
+        own_low[n] = jnp.where(lower, pltpu.roll(upper_rows, HALF, 1), lower_rows)
     pl.semaphore_wait(barrier, len(peers))
 
     mask_copies = []
@@ -139,19 +144,32 @@
             copy.start()
             mask_copies.append(copy)
     copies = {}
-    for g, (p, count) in enumerate(MESSAGES):
-        if g:
-            for n in range(p, p + count):
-                locals_[n].wait()
-        for d in range(REACH):
-            copy = pltpu.make_async_remote_copy(
-                src_ref=own_pack.at[pl.ds(p, count)],
-                dst_ref=got.at[d, pl.ds(p, count)],
-                send_sem=send_sem.at[d, g], recv_sem=recv_sem.at[d, g],
-                device_id=target(d), device_id_type=MESH,
-            )
-            copy.start()
-            copies[d, g] = copy
+    pieces = (
+        ((own_pack.at[pl.ds(0, 2)], lambda d: got.at[d, pl.ds(0, 2)]),),
+        (
+            (own_pack.at[3], lambda d: got.at[d, 3]),
+            (own_pack.at[2, pl.ds(0, HALF)], lambda d: got.at[d, 2, pl.ds(0, HALF)]),
+            (own_low.at[0], lambda d: got_low.at[d, 0]),
+        ),
+        (
+            (own_pack.at[4, pl.ds(0, HALF)], lambda d: got.at[d, 4, pl.ds(0, HALF)]),
+            (own_low.at[1], lambda d: got_low.at[d, 1]),
+        ),
+    )
+    sem_id = 0
+    for g, group in enumerate(pieces):
+        if g == 1:
+            locals_[3].wait()
+        for src, dst in group:
+            for d in range(REACH):
+                copy = pltpu.make_async_remote_copy(
+                    src_ref=src, dst_ref=dst(d),
+                    send_sem=send_sem.at[d, sem_id], recv_sem=recv_sem.at[d, sem_id],
+                    device_id=target(d), device_id_type=MESH,
+                )
+                copy.start()
+                copies.setdefault(g, []).append(copy)
+            sem_id += 1
     locals_[5].wait()
     sib_copy = pltpu.make_async_remote_copy(
         src_ref=own_rows, dst_ref=own_rows,
@@ -175,11 +193,14 @@
         edge = jnp.where(gap > 0, jnp.exp(-jnp.abs(gap).astype(F32) * rate), 0.0)
         edge_hi[r0 : r0 + 128, : 2 * BANDS], edge_lo[r0 : r0 + 128, : 2 * BANDS] = split(edge)
         side_lane = iota((128, 2 * BANDS), 1)
-        low_half = (side_lane + core) % 2 == 1
-        reach = jnp.where(low_half, TILE - 1 - pos, pos - TILE)
-        side_rate = 1.0 / (1 + (side_lane // 2) % CLASSES).astype(F32)
+        per_band = side_lane >= BANDS
+        odd = jnp.where(per_band, 1, side_lane % 2)
+        side_class = jnp.where(per_band, side_lane, side_lane // 2) % CLASSES
+        reach = jnp.where((odd + core) % 2 == 1, TILE - 1 - pos, pos - TILE)
+        side_rate = 1.0 / (1 + side_class).astype(F32)
+        used = per_band | (side_lane < 2 * CLASSES)
         spill = jnp.where(
-            (reach >= 0) & (side_lane < 2 * CLASSES), jnp.exp(-jnp.abs(reach).astype(F32) * side_rate), 0.0
+            (reach >= 0) & used, jnp.exp(-jnp.abs(reach).astype(F32) * side_rate), 0.0
         )
         edge_hi[r0 : r0 + 128, 2 * BANDS :], edge_lo[r0 : r0 + 128, 2 * BANDS :] = split(spill)
         decay = jnp.where(inside, jnp.exp(-jnp.abs(gap).astype(F32) * rate), 0.0)
@@ -242,10 +263,21 @@
     outer[...] = dot3((edge_t_hi[...], edge_t_lo[...]), panel)
     outer_decay[...] = dot3(split(outer[...]), decays)
 
+    near_half = pl.ds(first, TILE)
+    far_half = pl.ds(pl.multiple_of(TILE - first, TILE), TILE)
+    far_pos = iota((TILE, BANDS), 0)
+    far_dist = jnp.where(core == 0, far_pos + 1, TILE - far_pos).astype(F32)
+    far_rise = jnp.exp(-far_dist / (1 + iota((TILE, BANDS), 1) % CLASSES).astype(F32))
+    any_win = 0.0
+    for l in range(CLASSES):
+        start = pl.multiple_of(l * PANEL + TILE - first, TILE)
+        any_win = any_win + win[pl.ds(start, TILE), :].astype(F32)
+    far_rise = split(far_rise * any_win)
+    for lb in range(CLASSES):
+        filt_rise[lb] = dot3(split(filt[lb, :, far_half]), far_rise)
+    outer_rise[...] = dot3(split(outer[:, far_half]), far_rise)
     for copy in mask_copies:
         copy.wait()
-    total[...] = jnp.zeros_like(total)
-    boxes[...] = jnp.zeros_like(boxes)
     gram[...] = jnp.zeros_like(gram)
     mirror[...] = jnp.zeros_like(mirror)
     for d in range(REACH):
@@ -266,19 +298,30 @@
             out = out + got[d, p] * row_marks[d, r] * cols
         return out
 
+    def summed_square(p, n):
+        r, c = pack[p]
+        top = low = 0.0
+        for d in range(REACH):
+            cols = got_mask[d, :, lanes_of(c)].astype(F32)
+            low_cols = jnp.where(lower[:1], pltpu.roll(cols, HALF, 1), cols)
+            marks = row_marks[d, r]
+            low_marks = jnp.where(lower, marks[HALF : HALF + HALF // 2], marks[HALF + HALF // 2 :])
+            top = top + got[d, p, :HALF] * marks[:HALF] * cols
+            low = low + got_low[d, n] * low_marks * low_cols
+        square = jnp.concatenate((top, pltpu.roll(low, HALF, 1), low), axis=0)
+        row, lane_at = iota((BLOCK, BLOCK), 0), iota((BLOCK, BLOCK), 1)
+        return jnp.where((row >= HALF) & (lane_at < HALF), jnp.transpose(square), square)
+
     def filtered(rows, l):
         square = slice(l * PANEL, l * PANEL + TILE)
         return dot3(rows, (toep_hi[:TILE, square], toep_lo[:TILE, square]))
-
-    near_half = pl.ds(first, TILE)
-    far_half = pl.ds(pl.multiple_of(TILE - first, TILE), TILE)
 
     far_copy = pltpu.make_async_remote_copy(
         src_ref=far_sum, dst_ref=got_far,
         send_sem=far_sem.at[0], recv_sem=far_sem.at[1], device_id=sibling, device_id_type=MESH,
     )
-    for d in range(REACH):
-        copies[d, 0].wait_recv()
+    for copy in copies[0]:
+        copy.wait_recv()
     for r in range(2):
         far_sum[r] = summed(r)
     far_copy.start()
@@ -299,6 +342,22 @@
     stack = tuple(jnp.concatenate(pair, axis=0) for pair in ((rows[0], gram_hi), (rows[1], gram_lo)))
     for l in range(CLASSES):
         far_out[:, l * TILE : (l + 1) * TILE] = filtered(stack, l)
+    inside_all = jnp.concatenate([win_t[lb, :, near_half] for lb in range(CLASSES)], axis=1)
+    for la in range(CLASSES):
+        out = far_out[:ROWS, la * TILE : (la + 1) * TILE]
+        hi, lo = split(
+            jnp.concatenate([out * filt[lb, :, far_half] for lb in range(la, CLASSES)], axis=0)
+        )
+        above = inside_all[:, la * ROWS :]
+        rim = far_out[ROWS:, la * TILE : (la + 1) * TILE] * outer[:, far_half]
+        box = mm(above, hi) + mm(above, lo) - (rim[:BANDS] + rim[BANDS:])
+        boxes[:, la * TILE : (la + 1) * TILE] = box
+    far_fisher = jnp.zeros((BANDS, BANDS), F32)
+    for la in range(CLASSES):
+        hi, lo = split(boxes[:, la * TILE : (la + 1) * TILE])
+        channels = win[pl.ds(pl.multiple_of(la * PANEL + TILE - first, TILE), TILE), :]
+        far_fisher = far_fisher + (mm(hi, channels) + mm(lo, channels))
+    total[...] = far_fisher
 
     in_low = core == 0
     tile_lane = iota((1, TILE), 1).astype(F32)
@@ -306,17 +365,17 @@
     for l in range(CLASSES):
         to_low = jnp.exp((tile_lane - TILE) * (1.0 / (1 + l)))
         to_high = jnp.exp((tile_lane + 1.0) * (-1.0 / (1 + l)))
-        rises.append((jnp.where(in_low, to_low, to_high), jnp.where(in_low, to_high, to_low)))
+        rises.append(jnp.where(in_low, to_low, to_high))
     for k in range(2):
         y0 = k * BLOCK
-        for d in range(REACH):
-            copies[d, k + 1].wait_recv()
+        for copy in copies[k + 1]:
+            copy.wait_recv()
         if k == 0:
             corner = summed(3)
-            blocks = (summed(2), corner)
+            blocks = (summed_square(2, 0), corner)
             turned_corner[...] = jnp.transpose(corner)
         else:
-            blocks = (turned_corner[...], summed(4))
+            blocks = (turned_corner[...], summed_square(4, 1))
         rows = split(jnp.concatenate(blocks, axis=1))
         here = pl.ds(pl.multiple_of(first + y0, BLOCK), BLOCK)
         decay_t = (decay_t_hi[:, here], decay_t_lo[:, here])
@@ -330,40 +389,37 @@
         rims = []
         for lb in range(CLASSES):
             rim = edges[:, : 2 * BANDS] * filt_edge[lb, y0 : y0 + BLOCK, :]
-            rims.append(rim[:, :BANDS] + rim[:, BANDS:])
+            spilt = edges[:, 3 * BANDS :] * filt_rise[lb, y0 : y0 + BLOCK, :]
+            rims.append(rim[:, :BANDS] + rim[:, BANDS:] - spilt)
         inside = jnp.concatenate([win_t[lb, :, here] for lb in range(CLASSES)], axis=1)
         hi, lo = split(jnp.concatenate(rims, axis=0))
         total[...] -= mm(inside, hi) + mm(inside, lo)
         for la in range(CLASSES):
             near_out = filtered(stack, la)
             above = inside[:, la * BLOCK :]
-            tile = slice(la * TILE, (la + 1) * TILE)
-            for j, half_cols in enumerate((near_half, far_half)):
-                lane_col = 2 * BANDS + 2 * la + j
-
-                def square(own, far_rows, source):
-                    plain = near_out[own : own + BLOCK] if j == 0 else far_out[far_rows, tile]
-                    return plain + source[:, lane_col : lane_col + 1] * rises[la][j]
-
-                out = square(0, slice(y0, y0 + BLOCK), edges)
-                hi, lo = split(
-                    jnp.concatenate(
-                        [out * filt[lb, y0 : y0 + BLOCK, half_cols] for lb in range(la, CLASSES)],
-                        axis=0,
-                    )
+            step_up = rises[la]
+            lane_col = 2 * BANDS + 2 * la
+            out = near_out[:BLOCK] + edges[:, lane_col : lane_col + 1] * step_up
+            hi, lo = split(
+                jnp.concatenate(
+                    [out * filt[lb, y0 : y0 + BLOCK, near_half] for lb in range(la, CLASSES)], axis=0
                 )
-                box = mm(above, hi) + mm(above, lo)
-                if k == 1:
-                    rim = square(BLOCK, slice(2 * BLOCK, 3 * BLOCK), mirror[...]) * outer[:, half_cols]
-                    box = box - (rim[:BANDS] + rim[BANDS:])
-                span = slice(la * PANEL + j * TILE, la * PANEL + (j + 1) * TILE)
-                boxes[:, span] += box
+            )
+            box = mm(above, hi) + mm(above, lo)
+            span = slice(la * TILE, (la + 1) * TILE)
+            if k == 0:
+                boxes[:, span] = box
+            else:
+                rim = near_out[BLOCK:] + mirror[:, lane_col : lane_col + 1] * step_up
+                rim = rim * outer[:, near_half]
+                boxes[:, span] += box - (rim[:BANDS] + rim[BANDS:])
     fisher = total[...]
     for la in range(CLASSES):
-        for j, half_first in enumerate((first, TILE - first)):
-            hi, lo = split(boxes[:, la * PANEL + j * TILE : la * PANEL + (j + 1) * TILE])
-            channels = win[pl.ds(pl.multiple_of(la * PANEL + half_first, TILE), TILE), :]
-            fisher = fisher + (mm(hi, channels) + mm(lo, channels))
+        hi, lo = split(boxes[:, la * TILE : (la + 1) * TILE])
+        channels = win[pl.ds(pl.multiple_of(la * PANEL + first, TILE), TILE), :]
+        fisher = fisher + (mm(hi, channels) + mm(lo, channels))
+    over = mirror[:, 3 * BANDS :] * outer_rise[...]
+    fisher = fisher - (over[:BANDS] + over[BANDS:])
     four = mirror[:, : 2 * BANDS] * outer_decay[...]
     fisher = fisher + (four[:BANDS, :BANDS] + four[:BANDS, BANDS:])
     fisher = fisher + (four[BANDS:, :BANDS] + four[BANDS:, BANDS:])
@@ -430,7 +486,7 @@
             one = jnp.where(lanes == band + side * BANDS, line, 0.0)
             out_ref[h, :, side : side + 1] = jnp.sum(one, axis=1, keepdims=True)
 
-    for copy in list(copies.values()) + [far_copy] + xy_copies + z_copies:
+    for copy in copies[0] + copies[1] + copies[2] + [far_copy] + xy_copies + z_copies:
         copy.wait_send()
 
 
@@ -453,7 +509,9 @@
             vmem((2, BANDS), jnp.int32),
             vmem((PANEL, PANEL), F32),
             vmem((5, BLOCK, BLOCK), F32),
+            vmem((2, HALF // 2, BLOCK), F32),
             vmem((REACH, 5, BLOCK, BLOCK), F32),
+            vmem((REACH, 2, HALF // 2, BLOCK), F32),
             vmem((REACH, 1, 2 * PANEL), jnp.int32),
             vmem((REACH, 1, 2), jnp.int32),
             vmem((REACH, 2, BLOCK, BLOCK), F32),
@@ -461,6 +519,8 @@
             vmem((2, BLOCK, BLOCK), F32),
             vmem((ROWS, 4 * BANDS), F32),
             vmem((ROWS + 2 * BANDS, CLASSES * TILE), F32),
+            vmem((CLASSES, ROWS, BANDS), F32),
+            vmem((2 * BANDS, BANDS), F32),
             vmem((BLOCK, BLOCK), F32),
             vmem((ROWS, TILE), BF16),
             vmem((ROWS, TILE), BF16),
@@ -482,7 +542,7 @@
             vmem((CLASSES, ROWS, 2 * BANDS), F32),
             vmem((2 * BANDS, PANEL), F32),
             vmem((2 * BANDS, 2 * BANDS), F32),
-            vmem((BANDS, CLASSES * PANEL), F32),
+            vmem((BANDS, CLASSES * TILE), F32),
             vmem((2 * BANDS, TILE), F32),
             vmem((BANDS, BANDS), F32),
             vmem((2 * BANDS, 4 * BANDS), F32),
@@ -490,8 +550,8 @@
             vmem((15, 2, 128), F32),
             vmem((2, 1, 128), F32),
             vmem((7, 1, 128), F32),
-            dma((REACH, len(MESSAGES))),
-            dma((REACH, len(MESSAGES))),
+            dma((REACH, 6)),
+            dma((REACH, 6)),
             dma((2, REACH)),
             dma((2, REACH)),
             dma((2,)),

time: 40.1 us -> 39.6 us (0.988)
  Pallas kernels: 39.3 us -> 38.8 us
    pallas_call x1, Pallas kernels: 39.3 us -> 38.8 us  [body(): pl.pallas_call(body_kernel, out_shape=jax.ShapeDtypeStruct((2, 16, 2), F3...]
where the time goes in v6:
time: 39.6 us; the launch traced here: 39.5 us
  Pallas kernels  38.8 us (98%)
  local copies, waits for them, and re-layouts  0.66 us (2%)
    pallas_call x1, Pallas kernels, body(): pl.pallas_call(body_kernel, out_shape=jax.ShapeDtypeStruct((2, 16, 2), F3...  38.8 us

profile of v6, /device:TPU:1, one launch (start us, length us, event | category | flops | bytes accessed | tf_op | source)
XLA Modules:
  0.0 39.5 jit_solution(14141568713103491090)
XLA Ops:
  0.0 38.8 %shard_map.46 = f32[2,16,2]{2,1,0:T(8,128)S(1)} custom-call(f32[1,256,1024]{2,1,0:T(8,128)} %inv_ref.1, s32[1,1024]{1,0:T(1,128)} %mask_hbm.1, s32[1,2]{1,0:T(1,128)} %partner_hbm.1, s32[2,64]{1,0:T(2,128)} %start_hbm.1), custom_call_target="tpu_custom_call" | custom-call | tf_op jit(solution)/shard_map/pallas_call | solution.py:496
  38.8 0.7 %copy.5 = f32[2,16,2]{1,2,0:T(2,128)} copy(f32[2,16,2]{2,1,0:T(8,128)S(1)} %shard_map.46) | data formatting | bytes 512 | tf_op jit(solution)/shard_map/pallas_call | solution.py:496

commit v7 on v6

--- a/solution.py
+++ b/solution.py
@@ -46,6 +46,14 @@
 
 def down(row, count):
     return jnp.transpose(jnp.broadcast_to(row, (128, count)))
+
+
+def band_at(place):
+    return 2 * ((place % 2) * 16 + (place % 32) // 2) + (place // 32) % 2
+
+
+def class_at(place):
+    return 2 * ((place // 2) % 2) + (place // 32) % 2
 
 
 def body_kernel(
@@ -180,8 +188,12 @@
     locals_[8].wait()
     starts = start_ref[pl.ds(half, 1), :]
     starts2 = jnp.concatenate([starts, starts], axis=1)
+    square = (2 * BANDS, 2 * BANDS)
+    in_place = iota(square, 0) == band_at(iota(square, 1))
+    by_band = down(starts2.astype(F32), 2 * BANDS)
+    starts2 = jnp.sum(jnp.where(in_place, by_band, 0.0), axis=0, keepdims=True).astype(jnp.int32)
     lane = iota((1, 2 * BANDS), 1)
-    lane_class = lane % CLASSES
+    lane_class = class_at(lane)
     rate = 1.0 / (1 + lane_class).astype(F32)
     is_left = lane < BANDS
     for r0 in range(0, PANEL, 128):
@@ -195,7 +207,7 @@
         side_lane = iota((128, 2 * BANDS), 1)
         per_band = side_lane >= BANDS
         odd = jnp.where(per_band, 1, side_lane % 2)
-        side_class = jnp.where(per_band, side_lane, side_lane // 2) % CLASSES
+        side_class = jnp.where(per_band, class_at(side_lane), side_lane // 2 % CLASSES)
         reach = jnp.where((odd + core) % 2 == 1, TILE - 1 - pos, pos - TILE)
         side_rate = 1.0 / (1 + side_class).astype(F32)
         used = per_band | (side_lane < 2 * CLASSES)
@@ -210,7 +222,7 @@
             win[l * PANEL + r0 : l * PANEL + r0 + 128, :] = one.astype(BF16)
     starts_t = down(starts2.astype(F32), 2 * BANDS).astype(jnp.int32)
     sub = iota((2 * BANDS, 128), 0)
-    sub_class = sub % CLASSES
+    sub_class = class_at(sub)
     rate_t = 1.0 / (1 + sub_class).astype(F32)
     is_left_t = sub < BANDS
     for r0 in range(0, PANEL, 128):
@@ -267,7 +279,7 @@
     far_half = pl.ds(pl.multiple_of(TILE - first, TILE), TILE)
     far_pos = iota((TILE, BANDS), 0)
     far_dist = jnp.where(core == 0, far_pos + 1, TILE - far_pos).astype(F32)
-    far_rise = jnp.exp(-far_dist / (1 + iota((TILE, BANDS), 1) % CLASSES).astype(F32))
+    far_rise = jnp.exp(-far_dist / (1 + class_at(iota((TILE, BANDS), 1))).astype(F32))
     any_win = 0.0
     for l in range(CLASSES):
         start = pl.multiple_of(l * PANEL + TILE - first, TILE)
@@ -423,27 +435,14 @@
     four = mirror[:, : 2 * BANDS] * outer_decay[...]
     fisher = fisher + (four[:BANDS, :BANDS] + four[:BANDS, BANDS:])
     fisher = fisher + (four[BANDS:, :BANDS] + four[BANDS:, BANDS:])
-    row_class = iota((BANDS, BANDS), 0) % CLASSES
-    col_class = iota((BANDS, BANDS), 1) % CLASSES
+    row_class = class_at(iota((BANDS, BANDS), 0))
+    col_class = class_at(iota((BANDS, BANDS), 1))
     kept = jnp.where(col_class <= row_class, fisher * SCALE, 0.0)
     wide = jnp.concatenate([kept, jnp.zeros_like(kept)], axis=1)
     turned_over = jnp.transpose(jnp.concatenate([wide, jnp.zeros_like(wide)], axis=0))
     fisher = kept + jnp.where(col_class > row_class, turned_over[:BANDS, :BANDS], 0.0)
 
-    row = iota((BANDS // 2, BANDS), 0)
-    owner = (row % 2) * 16 + row // 2
-    col = iota((BANDS // 2, BANDS), 1)
-    parts3 = []
-    rest = fisher
-    for _ in range(3):
-        piece = rest.astype(BF16)
-        parts3.append(piece)
-        rest = rest - piece.astype(F32)
-    turned = []
-    for side in range(2):
-        pick = jnp.where(col == 2 * owner + side, 1.0, 0.0).astype(BF16)
-        turned.append(mm(pick, parts3[0]) + mm(pick, parts3[1]) + mm(pick, parts3[2]))
-    placed = jnp.concatenate(turned, axis=1)
+    placed = jnp.concatenate([fisher[: BANDS // 2], fisher[BANDS // 2 :]], axis=1)
     for j in range(16):
         sum_xy[j] = placed[2 * j : 2 * j + 2]
 
@@ -480,6 +479,7 @@
             halves[h] = halves[h] + jnp.where(from_half == h, got_z[e], 0.0)
     lanes = iota((16, 128), 1)
     band = 16 * part + iota((16, 128), 0)
+    band = 32 * (band % 2) + 2 * (band // 2 % 16) + band // 32
     for h in range(2):
         line = jnp.broadcast_to(halves[h], (16, 128))
         for side in range(2):

time: 39.6 us -> 39.4 us (level)
  no operation moved by 1% of the time
where the time goes in v7:
time: 39.4 us; the launch traced here: 39.3 us
  Pallas kernels  38.7 us (98%)
  local copies, waits for them, and re-layouts  0.66 us (2%)
    pallas_call x1, Pallas kernels, body(): pl.pallas_call(body_kernel, out_shape=jax.ShapeDtypeStruct((2, 16, 2), F3...  38.7 us

profile of v7, /device:TPU:1, one launch (start us, length us, event | category | flops | bytes accessed | tf_op | source)
XLA Modules:
  0.0 39.3 jit_solution(11538077093921637833)
XLA Ops:
  0.0 38.7 %shard_map.46 = f32[2,16,2]{2,1,0:T(8,128)S(1)} custom-call(f32[1,256,1024]{2,1,0:T(8,128)} %inv_ref.1, s32[1,1024]{1,0:T(1,128)} %mask_hbm.1, s32[1,2]{1,0:T(1,128)} %partner_hbm.1, s32[2,64]{1,0:T(2,128)} %start_hbm.1), custom_call_target="tpu_custom_call" | custom-call | tf_op jit(solution)/shard_map/pallas_call | solution.py:496
  38.7 0.7 %copy.5 = f32[2,16,2]{1,2,0:T(2,128)} copy(f32[2,16,2]{2,1,0:T(8,128)S(1)} %shard_map.46) | data formatting | bytes 512 | tf_op jit(solution)/shard_map/pallas_call | solution.py:496
